TPU v7x, 512 devices: a whole 4x4x16 slice. The times are simulated.
512 devices in a mesh: dp: 16 (over x_lo, y, core), vocab: 32 (over x_hi, z).
Axes of the slice: x: 4 (x_hi: 2, x_lo: 2; x = x_hi * 2 + x_lo), y: 4, z: 16, core: 2. Of those that a mesh axis runs over, the one named last changes fastest.
Arguments:
- student_hidden: bfloat16 [2048, 2048], P('dp', 'vocab'), may hold values from -210 to 210
- student_blocks: bfloat16 [32, 1024, 4864], P('vocab', 'dp'), may hold values from -0.375 to 0.375
- teacher_logits: bfloat16 [2048, 77824], P('dp', 'vocab'), may hold values from -16 to 308
- token_ids: int32 [2048], P('dp'), may hold values from 0 to 77823
- loss_mask: int32 [2048], P('dp'), may hold values from 0 to 1, as said below
Outputs:
- hidden_grad: bfloat16 [2048, 2048], P('dp', 'vocab')
- token_kl: float32 [2048], P('dp')
- sampled_logprob: float32 [2048], P('dp')
- loss: float32 [], replicated
Inputs may be any that keep to these rules, and one draw needn't show every extreme that they name: `loss_mask`: in each block of 128 tokens the mask is 0 on a leading run of at most 64 tokens and 1 on the rest.
All inputs are finite; a program needn't handle non-finite values.
Results may differ from a plain program's by a relative error of at most 0.0047.
Values may be sent and summed in bfloat16 or wider, within the bound.
A program may use at most 64 MiB of HBM per device.

v0:
```python
import jax
import jax.numpy as jnp
from jax import lax
from jax.sharding import Mesh
from jax.sharding import PartitionSpec as P

D = 2048
VT = 2432
VOCAB = ("vocab_0", "vocab_1")


def from_everyone(shard, axis):
    count = lax.axis_size(axis)
    return lax.all_to_all(
        jnp.broadcast_to(shard[None], (count, *shard.shape)), axis, 0, 0, tiled=True
    )


def taken_together(shard, axis):
    return from_everyone(shard, axis).sum(axis=0)


def laid_out(parts, dim):
    parts = jnp.moveaxis(parts, 0, dim)
    dims = parts.shape
    return parts.reshape(*dims[:dim], dims[dim] * dims[dim + 1], *dims[dim + 2 :])


def stacked_from(shard, axes, sequence):
    parts = shard[None]
    for k in sequence:
        parts = lax.all_gather(parts, axes[k], axis=0, tiled=True)
    current = [lax.axis_size(axes[k]) for k in reversed(sequence)]
    parts = parts.reshape(*current, *shard.shape)
    turned = sorted(range(len(sequence)), key=lambda place: sequence[len(sequence) - 1 - place])
    return parts.transpose(*turned, *range(len(sequence), parts.ndim)).reshape(-1, *shard.shape)


def gathered_by_axis(shard, axes, sequence, dim):
    return laid_out(stacked_from(shard, axes, sequence), dim)


def swapped(shard, axis, stride):
    return lax.ppermute(shard, axis, [(i, i ^ 1 << stride) for i in range(lax.axis_size(axis))])


def collected_together(shard, axis):
    leaves = jax.tree.leaves(shard)
    sequence = sorted(range(len(leaves)), key=lambda k: -leaves[k].size)
    width = (1, *leaves[sequence[0]].shape)[-1]
    lines = [
        jnp.pad(leaves[k].reshape(-1), (0, -leaves[k].size % width)).reshape(-1, width)
        for k in sequence
    ]
    both, at, found = (from_everyone(jnp.concatenate(lines), axis), 0, {})
    for k, line in zip(sequence, lines):
        share = both[:, at : at + len(line)].reshape(len(both), -1)
        found[k] = share[:, : leaves[k].size].reshape(-1, *leaves[k].shape)
        at += len(line)
    numbers = iter(range(len(leaves)))
    return jax.tree.map(lambda _: found[next(numbers)], shard)


def folded_in_pairs(pieces, combine):
    while len(jax.tree.leaves(pieces)[0]) > 1:
        pieces = jax.vmap(combine)(
            *(jax.tree.map(lambda part: part[side::2], pieces) for side in (0, 1))
        )
    return jax.tree.map(lambda part: part[0], pieces)


def merged_2(shard, axis, combine):
    pieces = collected_together(shard, axis)
    return folded_in_pairs(pieces, combine)


def in_blocks(shard, dim, count):
    before, after = (shard.shape[:dim], shard.shape[dim + 1 :])
    return jnp.moveaxis(shard.reshape(*before, count, -1, *after), dim, 0)


def sum_at_owner(shard, axis, dim):
    parts = in_blocks(shard, dim, lax.axis_size(axis))
    arrived = lax.all_to_all(parts, axis, split_axis=0, concat_axis=0, tiled=True)
    return arrived.sum(axis=0)


def pair_merge(left_pair, right_pair):
    left_max, left_total = left_pair
    right_max, right_total = right_pair
    top_value = jnp.maximum(left_max, right_max)
    merged_total = left_total * jnp.exp(left_max - top_value) + right_total * jnp.exp(
        right_max - top_value
    )
    return (top_value, merged_total)


def double_merge(left_four, right_four):
    first_pair = pair_merge(left_four[0:2], right_four[0:2])
    second_pair = pair_merge(left_four[2:4], right_four[2:4])
    return first_pair + second_pair


def row_stats(values):
    row_max = jnp.max(values, axis=1)
    row_total = jnp.sum(jnp.exp(values - row_max[:, None]), axis=1)
    return (row_max, row_total)


def on_device(student_hidden, student_blocks, teacher_logits, token_ids, loss_mask):
    vocab_index = lax.axis_index(VOCAB)
    pair_side = vocab_index % 2
    mask_float = loss_mask.astype(jnp.float32)
    mask_total = taken_together(jnp.sum(mask_float), "dp")
    gathered = gathered_by_axis(student_hidden, VOCAB, (0, 1), 1)
    piece = student_blocks[0]
    own_block = lax.dynamic_slice_in_dim(piece, pair_side * VT, VT, 1)
    far_block = lax.dynamic_slice_in_dim(piece, (1 - pair_side) * VT, VT, 1)
    received = swapped(far_block, VOCAB, 0)
    stacked = jnp.where(
        pair_side == 0, jnp.stack([own_block, received]), jnp.stack([received, own_block])
    )
    weight = lax.all_gather(stacked, "dp", axis=1, tiled=True).reshape(D, VT)
    logits = jnp.dot(gathered, weight, preferred_element_type=jnp.float32)
    column_start = vocab_index * VT
    teacher_local = teacher_logits.astype(jnp.float32)
    teacher_max, teacher_total = row_stats(teacher_local)
    student_max, student_total = row_stats(logits)
    merged = merged_2((teacher_max, teacher_total, student_max, student_total), VOCAB, double_merge)
    stats = (merged[0], merged[1], merged[2], merged[3])
    teacher_logp = teacher_local - stats[0][:, None] - jnp.log(stats[1])[:, None]
    student_logp = logits - stats[2][:, None] - jnp.log(stats[3])[:, None]
    teacher_prob = jnp.exp(teacher_logp)
    kl_part = jnp.sum(teacher_prob * (teacher_logp - student_logp), axis=1)
    columns = lax.broadcasted_iota(jnp.int32, logits.shape, 1) + column_start
    sampled_part = jnp.sum(jnp.where(columns == token_ids[:, None], student_logp, 0.0), axis=1)
    token_kl, sampled = (taken_together(kl_part, VOCAB), taken_together(sampled_part, VOCAB))
    loss = taken_together(jnp.sum(mask_float * token_kl), "dp") / mask_total
    factor = mask_float / mask_total
    dlogits = (factor[:, None] * (jnp.exp(student_logp) - teacher_prob)).astype(jnp.bfloat16)
    term = lax.dot_general(
        dlogits, weight, (((1,), (1,)), ((), ())), preferred_element_type=jnp.float32
    )
    hidden_grad = sum_at_owner(term, VOCAB, 1).astype(jnp.bfloat16)
    return (hidden_grad, token_kl, sampled, loss)


def solution(mesh):
    finer = Mesh(mesh.devices.reshape(mesh.shape["dp"], 2, 16), ("dp", "vocab_0", "vocab_1"))
    return jax.shard_map(
        on_device,
        mesh=finer,
        in_specs=(P("dp", VOCAB), P(VOCAB, "dp", None), P("dp", VOCAB), P("dp"), P("dp")),
        out_specs=(P("dp", VOCAB), P("dp"), P("dp"), P()),
        check_vma=False,
    )
```

profile of v0, /device:TPU:34, one launch (start us, length us, event | category | flops | bytes accessed | tf_op | source)
XLA Modules:
  0.0 263.0 jit_solution(6947266901041951230)
XLA Ops:
  7.2 0.0 all-gather.3.cloned.1.call-start
  7.2 1.1 constant_dynamic-slice_fusion
  8.3 0.0 copy-start.1
  8.4 2.0 collective-permute-start
  10.4 9.0 %collective-permute-done = bf16[64,2432]{1,0:T(8,128)(2,1)S(1)} collective-permute-done((bf16[64,2432]{1,0:T(8,128)(2,1)S(1)}, bf16[64,2432]{1,0:T(8,128)(2,1)S(1)}, u32[]{:S(2)}, u32[]{:S(2)}) %collective-permute-start) | collective-permute-done | bytes 311328 | tf_op jit(solution)/shard_map/ppermute | solution.py:44
  19.4 0.9 maximum_select_fusion
  20.3 0.0 copy-start
  20.3 0.0 all-gather.3.cloned.1.call-update
  20.3 0.0 copy-done.1
  20.3 6.1 %all-gather = bf16[256,64]{0,1:T(8,128)(2,1)S(1)} all-gather(bf16[128,64]{0,1:T(8,128)(2,1)S(1)} %copy-done.1), channel_id=2, replica_groups=mesh['dp'=16,'vocab_0'=2,'vocab_1'=16] {'vocab_0'}, dimensions={0}, use_global_device_ids=true | all-gather | bytes 49152 | tf_op jit(solution)/shard_map/all_gather | solution.py:32
  26.4 36.5 %all_gather.11 = bf16[32,128,64]{1,2,0:T(8,128)(2,1)S(1)} all-gather(bf16[2,128,64]{1,2,0:T(8,128)(2,1)S(1)} %copy_bitcast_fusion), channel_id=1, replica_groups=mesh['dp'=16,'vocab_0'=2,'vocab_1'=16] {'vocab_1'}, dimensions={0}, use_global_device_ids=true | all-gather | bytes 557056 | tf_op jit(solution)/shard_map/all_gather | solution.py:32
  62.9 0.0 copy-done
  62.9 0.3 copy.35
  63.3 0.2 reduce_max.27
  63.4 0.3 fusion.1
  63.8 27.8 %all-gather.3.cloned.1.call-done = bf16[2,1024,2432]{2,1,0:T(8,128)(2,1)} async-done(((bf16[2,64,2432]{2,1,0:T(8,128)(2,1)}), bf16[2,1024,2432]{2,1,0:T(8,128)(2,1)}) %all-gather.3.cloned.1.call-update) | async-done | bytes 9961488 | tf_op jit(solution)/shard_map/all_gather | solution.py:123
  91.6 6.6 %fusion.19 = (f32[128]{0:T(128)S(1)}, f32[2432,128]{1,0:T(8,128)S(1)}) fusion(bf16[2048,2432]{1,0:T(8,128)(2,1)} %bitcast.60, bf16[128,2048]{0,1:T(8,128)(2,1)S(1)} %bitcast.63), kind=kOutput, calls=%fused_computation.47 | convolution fusion | flops 1275379584 | bytes 11731456 | tf_op jit(solution)/shard_map/dot_general | solution.py:124
  98.2 0.0 copy-start.3
  98.2 0.3 exponential_reduce_fusion
  98.6 0.6 broadcast_in_dim.18
  99.2 14.3 %all-to-all-start.1 = ((f32[32,4,128]{2,1,0:T(4,128)}), f32[32,4,128]{2,1,0:T(4,128)S(1)}, u32[]{:S(2)}, u32[]{:S(2)}) async-start(f32[32,4,128]{2,1,0:T(4,128)} %broadcast_in_dim.18), calls=%async_computation.1 | async-start | bytes 131072 | tf_op jit(solution)/shard_map/all_to_all | solution.py:14
  113.5 15.0 %all-to-all-done.1 = f32[32,4,128]{2,1,0:T(4,128)S(1)} async-done(((f32[32,4,128]{2,1,0:T(4,128)}), f32[32,4,128]{2,1,0:T(4,128)S(1)}, u32[]{:S(2)}, u32[]{:S(2)}) %all-to-all-start.1) | async-done | bytes 65568 | tf_op jit(solution)/shard_map/all_to_all | solution.py:14
  128.6 0.0 copy-start.4
  129.3 0.0 copy-done.3
  129.3 1.1 fusion.10
  130.4 17.7 %all_to_all.34 = f32[32,1,128]{2,1,0:T(1,128)S(1)} all-to-all(f32[32,1,128]{2,1,0:T(1,128)S(1)} %broadcast_in_dim.19), channel_id=1, replica_groups=mesh['dp'=16,'vocab_0'=2,'vocab_1'=16] {'vocab_0','vocab_1'}, dimensions={0} | all-to-all | bytes 32768 | tf_op jit(solution)/shard_map/all_to_all | solution.py:14
  148.2 0.0 copy-done.4
  148.2 0.0 copy-start.2
  148.2 0.6 multiply_reduce_fusion
  148.8 0.6 broadcast_in_dim.16
  149.4 10.1 %all_to_all.35 = f32[16,1,1]{2,1,0:T(1,128)S(1)} all-to-all(f32[16,1,1]{2,1,0:T(1,128)S(1)} %broadcast_in_dim.16), channel_id=1, replica_groups=mesh['dp'=16,'vocab_0'=2,'vocab_1'=16] {'dp'}, dimensions={0} | all-to-all | bytes 128 | tf_op jit(solution)/shard_map/all_to_all | solution.py:14
  159.5 0.6 broadcast_in_dim.21
  160.1 5.1 %all-to-all-start.4 = ((f32[32,1,128]{2,1,0:T(1,128)}), f32[32,1,128]{2,1,0:T(1,128)S(1)}, u32[]{:S(2)}, u32[]{:S(2)}) async-start(f32[32,1,128]{2,1,0:T(1,128)} %broadcast_in_dim.21), calls=%async_computation.4 | async-start | bytes 32768 | tf_op jit(solution)/shard_map/all_to_all | solution.py:14
  165.2 0.6 reduce_sum.100
  165.8 0.5 convert_divide_fusion
  166.3 12.4 %all-to-all-done.4 = f32[32,1,128]{2,1,0:T(1,128)S(1)} async-done(((f32[32,1,128]{2,1,0:T(1,128)}), f32[32,1,128]{2,1,0:T(1,128)S(1)}, u32[]{:S(2)}, u32[]{:S(2)}) %all-to-all-start.4) | async-done | bytes 16416 | tf_op jit(solution)/shard_map/all_to_all | solution.py:14
  178.7 1.2 broadcast_in_dim.22
  180.0 4.8 %all-to-all-start.5 = ((f32[16,1,1]{2,1,0:T(1,128)}), f32[16,1,1]{2,1,0:T(1,128)S(1)}, u32[]{:S(2)}, u32[]{:S(2)}) async-start(f32[16,1,1]{2,1,0:T(1,128)} %broadcast_in_dim.22), calls=%async_computation.5 | async-start | bytes 16384 | tf_op jit(solution)/shard_map/all_to_all | solution.py:14
  184.7 7.7 %convolution_bitcast_fusion = f32[32,128,64]{1,2,0:T(8,128)} fusion(bf16[32,64,2432]{2,1,0:T(8,128)(2,1)} %bitcast.61, bf16[128,2432]{0,1:T(8,128)(2,1)S(1)} %copy.35, f32[2432,128]{1,0:T(8,128)S(1)} %get-tuple-element.37, f32[128]{0:T(128)S(1)} %get-tuple-element.33, f32[128]{0:T(128)S(1)} %get-tuple-element.32, f32[128]{0:T(128)S(1)} %get-tuple-element.38, ...), kind=kOutput, calls=%fused_computation.2 | convolution fusion | flops 1277558784 | bytes 12880384 | tf_op jit(solution)/shard_map/dot_general | solution.py:141
  192.5 0.0 copy-done.2
  192.5 0.0 all-to-all-done.5
  192.5 5.2 %all-to-all-start.2 = ((f32[32,128,64]{1,2,0:T(8,128)}), f32[32,128,64]{1,2,0:T(8,128)S(1)}, u32[]{:S(2)}, u32[]{:S(2)}) async-start(f32[32,128,64]{1,2,0:T(8,128)} %convolution_bitcast_fusion), calls=%async_computation.2 | async-start | bytes 2097152 | tf_op jit(solution)/shard_map/all_to_all | solution.py:84
  197.7 0.5 reduce_sum.107
  198.2 0.6 reduce_sum.109
  200.1 54.3 %all-to-all-done.2 = f32[32,128,64]{1,2,0:T(8,128)S(1)} async-done(((f32[32,128,64]{1,2,0:T(8,128)}), f32[32,128,64]{1,2,0:T(8,128)S(1)}, u32[]{:S(2)}, u32[]{:S(2)}) %all-to-all-start.2) | async-done | bytes 1048608 | tf_op jit(solution)/shard_map/all_to_all | solution.py:84
  254.4 0.7 reduce_sum.103
  (49 shorter events, 0.7 us)
Async XLA Ops:
  7.2 84.4 %all-gather.3.cloned.1.call-start = ((), (), s32[]{:S(2)}) async-start(), calls=%async_computation.6 | async-start | bytes 10584064 | tf_op jit(solution)/shard_map/all_gather | solution.py:123
  8.3 11.9 %copy-start.1 = (bf16[128,64]{0,1:T(8,128)(2,1)S(1)}, bf16[128,64]{0,1:T(8,128)(2,1)}, u32[]{:S(2)}) copy-start(bf16[128,64]{0,1:T(8,128)(2,1)} %param.5) | copy-start | bytes 49156
  8.4 11.0 %collective-permute-start = (bf16[64,2432]{1,0:T(8,128)(2,1)S(1)}, bf16[64,2432]{1,0:T(8,128)(2,1)S(1)}, u32[]{:S(2)}, u32[]{:S(2)}) collective-permute-start(bf16[64,2432]{1,0:T(8,128)(2,1)S(1)} %get-tuple-element.25), channel_id=1, source_target_pairs={{0,1},{1,0},{2,3},{3,2},{4,5},{5,4},{6,7},{7,6},{8,9},{9,8},{10,11... | collective-permute-start | bytes 933896 | tf_op jit(solution)/shard_map/ppermute | solution.py:44
  20.3 42.7 %copy-start = (bf16[128,2432]{1,0:T(8,128)(2,1)S(1)}, bf16[128,2432]{1,0:T(8,128)(2,1)}, u32[]{:S(2)}) copy-start(bf16[128,2432]{1,0:T(8,128)(2,1)} %param.7) | copy-start | bytes 1867780
  98.2 31.1 %copy-start.3 = (s32[128]{0:T(128)S(1)}, s32[128]{0:T(128)}, u32[]{:S(2)}) copy-start(s32[128]{0:T(128)} %param.8) | copy-start | bytes 1540
  99.2 29.3 %all-to-all-start.1 = ((f32[32,4,128]{2,1,0:T(4,128)}), f32[32,4,128]{2,1,0:T(4,128)S(1)}, u32[]{:S(2)}, u32[]{:S(2)}) async-start(f32[32,4,128]{2,1,0:T(4,128)} %broadcast_in_dim.18), calls=%async_computation.1 | async-start | bytes 131072 | tf_op jit(solution)/shard_map/all_to_all | solution.py:14
  128.6 19.6 %copy-start.4 = (s32[128]{0:T(128)S(1)}, s32[128]{0:T(128)}, u32[]{:S(2)}) copy-start(s32[128]{0:T(128)} %param.9) | copy-start | bytes 1540
  148.2 44.3 %copy-start.2 = (f32[128]{0:T(128)}, f32[128]{0:T(128)S(1)}, u32[]{:S(2)}) copy-start(f32[128]{0:T(128)S(1)} %reduce_sum.105) | copy-start | bytes 1540
  160.1 18.6 %all-to-all-start.4 = ((f32[32,1,128]{2,1,0:T(1,128)}), f32[32,1,128]{2,1,0:T(1,128)S(1)}, u32[]{:S(2)}, u32[]{:S(2)}) async-start(f32[32,1,128]{2,1,0:T(1,128)} %broadcast_in_dim.21), calls=%async_computation.4 | async-start | bytes 32768 | tf_op jit(solution)/shard_map/all_to_all | solution.py:14
  180.0 12.5 %all-to-all-start.5 = ((f32[16,1,1]{2,1,0:T(1,128)}), f32[16,1,1]{2,1,0:T(1,128)S(1)}, u32[]{:S(2)}, u32[]{:S(2)}) async-start(f32[16,1,1]{2,1,0:T(1,128)} %broadcast_in_dim.22), calls=%async_computation.5 | async-start | bytes 16384 | tf_op jit(solution)/shard_map/all_to_all | solution.py:14
  192.5 61.9 %all-to-all-start.2 = ((f32[32,128,64]{1,2,0:T(8,128)}), f32[32,128,64]{1,2,0:T(8,128)S(1)}, u32[]{:S(2)}, u32[]{:S(2)}) async-start(f32[32,128,64]{1,2,0:T(8,128)} %convolution_bitcast_fusion), calls=%async_computation.2 | async-start | bytes 2097152 | tf_op jit(solution)/shard_map/all_to_all | solution.py:84
Sparse Core Ops, SparseCore 0:
  20.4 71.1 all-gather.2
where the time goes:
time: 264 us; the launch traced here: 263 us
  waiting for transfers between devices  118 us (45%)
  blocking collectives  70.4 us (27%)
  starting transfers between devices  31.4 us (12%)
  between operations  16.7 us (6%)
  matrix products  14.4 us (5%)
  other arithmetic  6.63 us (3%)
  local copies, waits for them, and re-layouts  5.18 us (2%)
    all_to_all x1, waiting for transfers between devices, sum_at_owner(): lax.all_to_all(parts, axis, split_axis=0, concat_axis=0, tiled=True)  54.3 us
    all_gather x2, blocking collectives, stacked_from(): parts = lax.all_gather(parts, axes[k], axis=0, tiled=True)  42.6 us
    all_to_all x2, blocking collectives, from_everyone(): lax.all_to_all(jnp.broadcast_to(shard[None], (count, *shard.shape)), axis...  27.8 us
    all_gather x1, waiting for transfers between devices, on_device(): weight = lax.all_gather(stacked, 'dp', axis=1, tiled=True).reshape(D, VT)  27.8 us
    all_to_all x3, waiting for transfers between devices, from_everyone(): lax.all_to_all(jnp.broadcast_to(shard[None], (count, *shard.shape)), axis...  27.3 us
    all_to_all x3, starting transfers between devices, from_everyone(): lax.all_to_all(jnp.broadcast_to(shard[None], (count, *shard.shape)), axis...  24.1 us
    ppermute x1, waiting for transfers between devices, swapped(): lax.ppermute(shard, axis, [(i, i ^ 1 << stride) for i in range(lax.axis_s...  8.96 us
    dot_general x1, matrix products, on_device(): lax.dot_general(dlogits, weight, (((1,), (1,)), ((), ())), preferred_elem...  7.74 us
  transfers between devices with their start and end apart: 6, of which 5 were waited for; matrix products, arithmetic and copies ran while one was open for 4% of the time, Pallas kernels for 0%

commit v1 on v0

v1 whole, which is shorter than its diff:
```python
import jax
import jax.numpy as jnp
from jax import lax
from jax.experimental import pallas as pl
from jax.experimental.pallas import tpu as pltpu
from jax.sharding import PartitionSpec as P

F32 = jnp.float32
BF16 = jnp.bfloat16
D = 2048
VT = 2432
TOK = 128
R = 64
NT = VT // 128
NZ = 16
MESH = pl.DeviceIdType.MESH

XP, YP, YM, ZP, CP = range(5)


def kernel(
    hid_ref, blk_ref, tea_ref, ids_ref, mask_ref,
    grad_ref, kl_ref, samp_ref, loss_ref,
    w, ht, hg, acc, lt, tt, et, dl, stat, mrow, lrow, xsend, xrecv, own, zsend, zrecv,
    w_send, w_recv, d_send, d_recv, loc_sem, h_send, h_recv,
    s_send, s_recv, m_send, m_recv, l_send, l_recv, x_send, x_recv, z_send, z_recv,
):
    d = lax.axis_index("dp")
    v = lax.axis_index("vocab")
    xl, y, c = d // 8, (d // 2) % 4, d % 2
    xh, z = v // NZ, v % NZ
    h = v % 2

    def dev(dp, vocab):
        return {"dp": dp, "vocab": vocab}

    target = {
        XP: dev(d ^ 8, v),
        YP: dev(xl * 8 + ((y + 1) % 4) * 2 + c, v),
        YM: dev(xl * 8 + ((y + 3) % 4) * 2 + c, v),
        ZP: dev(d, v ^ 1),
        CP: dev(d ^ 1, v),
    }
    far = [8, 7, 9, 6, 10, 5, 11, 4, 12, 3, 13, 2, 14, 1, 15]

    barrier = pltpu.get_barrier_semaphore()
    for r in range(1, 32):
        pl.semaphore_signal(barrier, inc=1, device_id=dev(d, v ^ r), device_id_type=MESH)
    for r in range(1, 16):
        pl.semaphore_signal(barrier, inc=1, device_id=dev(d ^ r, v), device_id_type=MESH)
    pl.semaphore_wait(barrier, 46)

    started = []

    def send(src, dst, ssem, rsem, to):
        copy = pltpu.make_async_remote_copy(
            src_ref=src, dst_ref=dst, send_sem=ssem, recv_sem=rsem, device_id=to, device_id_type=MESH
        )
        copy.start()
        started.append(copy)

    def arrived(dst, sem):
        pltpu.make_async_copy(dst, dst, sem).wait()

    def rows_of(t, dx, dy, core, half=None):
        base = (h ^ t) * 1024 + R * ((xl ^ dx) * 8 + ((y + dy) % 4) * 2 + core)
        if half is None:
            return pl.ds(pl.multiple_of(base, R), R)
        return pl.ds(pl.multiple_of(base + 32 * half, 32), 32)

    counter = {"w": 0, "d": 0}

    def sem_index(t, dx, dy, half):
        base = (t * 2 + dx) * 5
        return base + (dy if dy < 2 else 2 + half if dy == 2 else 4)

    def pass_on(t, dx, dy, way, half=None, src=None):
        ref = w.at[rows_of(t, dx, dy, c, half)]
        if way == XP:
            at = (t, dx ^ 1, dy)
        elif way == YP:
            at = (t, dx, (dy + 3) % 4)
        elif way == YM:
            at = (t, dx, (dy + 1) % 4)
        k = counter["w"]
        counter["w"] += 1
        send(ref if src is None else src, ref, w_send.at[k], w_recv.at[sem_index(*at, half or 0)], target[way])

    def across(t, dx, dy, half=None, src=None):
        ref = w.at[rows_of(t, dx, dy, c, half)]
        k = counter["d"]
        counter["d"] += 1
        send(ref if src is None else src, ref, d_send.at[k], d_recv.at[sem_index(t, dx, dy, half or 0)], target[CP])

    def piece_in(t, dx, dy, half=None):
        arrived(w.at[rows_of(t, dx, dy, c, half)], w_recv.at[sem_index(t, dx, dy, half or 0)])

    def peer_in(t, dx):
        for dy in range(4):
            for half in (0, 1) if dy == 2 else (None,):
                arrived(w.at[rows_of(t, dx, dy, 1 - c, half)], d_recv.at[sem_index(t, dx, dy, half or 0)])

    near = blk_ref.at[:, pl.ds(pl.multiple_of(h * VT, 128), VT)]
    away = blk_ref.at[:, pl.ds(pl.multiple_of((1 - h) * VT, 128), VT)]
    shard = jnp.concatenate([hid_ref[...].astype(F32), jnp.zeros((TOK, 128 - R), F32)], axis=1)
    mine = pl.ds(pl.multiple_of(xh * R, R), R)
    theirs = pl.ds(pl.multiple_of((1 - xh) * R, R), R)
    ht[z, mine, :] = shard.T[:R].astype(BF16)
    mrow[d] = mask_ref[...].astype(F32)
    send(ht.at[z, mine], ht.at[z, mine], h_send.at[15], h_recv.at[1], dev(d, v ^ NZ))
    send(away, w.at[pl.ds(pl.multiple_of(h * 1024 + R * d, R), R)], w_send.at[19], w_recv.at[sem_index(1, 0, 0, 0)], target[ZP])
    pass_on(0, 0, 0, XP, src=near)
    pass_on(0, 0, 0, YP, src=near)
    pass_on(0, 0, 0, YM, src=near)
    across(0, 0, 0, src=near)
    place = pltpu.make_async_copy(near, w.at[rows_of(0, 0, 0, c)], loc_sem)
    place.start()
    for r in range(1, 16):
        send(mrow.at[d], mrow.at[d], m_send.at[r - 1], m_recv, dev(d ^ r, v))

    def turn_teacher(j, top):
        at = pl.ds(pl.multiple_of(j * 128, 128), 128)
        block = tea_ref[:, at].astype(F32).T
        tt[at, :] = block
        return jnp.maximum(top, block.reshape(16, 8, 128).max(axis=0))

    top = lax.fori_loop(0, NT, turn_teacher, jnp.full((8, 128), -jnp.inf, F32))
    t_max = top.max(axis=0, keepdims=True)

    def exp_teacher(j, total):
        at = pl.ds(pl.multiple_of(j * 128, 128), 128)
        e = jnp.exp(tt[at, :] - t_max)
        et[at, :] = e
        return total + e.reshape(16, 8, 128).sum(axis=0)

    t_sum = lax.fori_loop(0, NT, exp_teacher, jnp.zeros((8, 128), F32)).sum(axis=0, keepdims=True)

    arrived(ht.at[z, theirs], h_recv.at[1])
    for i, k in enumerate(far):
        send(ht.at[z], ht.at[z], h_send.at[i], h_recv.at[0], dev(d, xh * NZ + (z + k) % NZ))

    piece_in(0, 0, 3)
    pass_on(0, 0, 3, YP, half=0)
    pass_on(0, 0, 3, XP)
    across(0, 0, 3)
    piece_in(0, 0, 1)
    pass_on(0, 0, 1, YM, half=1)
    across(0, 0, 1)
    piece_in(1, 0, 0)
    pass_on(1, 0, 0, XP)
    pass_on(1, 0, 0, YP)
    pass_on(1, 0, 0, YM)
    across(1, 0, 0)
    pass_on(0, 0, 1, XP)
    piece_in(0, 1, 0)
    across(0, 1, 0)
    for half in (0, 1):
        piece_in(0, 0, 2, half)
        pass_on(0, 0, 2, XP, half=half)
        across(0, 0, 2, half)
    piece_in(0, 1, 3)
    across(0, 1, 3)
    piece_in(1, 0, 3)
    pass_on(1, 0, 3, YP, half=0)
    across(1, 0, 3)
    piece_in(1, 0, 1)
    pass_on(1, 0, 1, YM, half=1)
    across(1, 0, 1)
    piece_in(1, 1, 0)
    pass_on(1, 1, 0, YP)
    pass_on(1, 1, 0, YM)
    across(1, 1, 0)
    for half in (0, 1):
        piece_in(1, 0, 2, half)
        across(1, 0, 2, half)

    arrived(ht.at[pl.ds(0, 15)], h_recv.at[0])
    for g in range(4):
        part = ht[8 * (g % 2) : 8 * (g % 2) + 8, (g // 2) * R : (g // 2) * R + R, :]
        hg[g] = part.reshape(512, TOK).astype(F32).T.astype(BF16)

    def multiply(t, dx, first):
        g = (h ^ t) * 2 + (xl ^ dx)
        rows = pl.ds(pl.multiple_of(g * 512, 512), 512)
        part = jnp.dot(hg[g], w[rows, :], preferred_element_type=F32)
        acc[...] = part if first else acc[...] + part

    place.wait()
    peer_in(0, 0)
    multiply(0, 0, True)
    piece_in(0, 1, 1)
    across(0, 1, 1)
    piece_in(1, 1, 3)
    pass_on(1, 1, 3, YP, half=0)
    across(1, 1, 3)
    piece_in(1, 1, 1)
    pass_on(1, 1, 1, YM, half=1)
    across(1, 1, 1)
    peer_in(1, 0)
    multiply(1, 0, False)
    for half in (0, 1):
        piece_in(1, 1, 2, half)
        across(1, 1, 2, half)
    for half in (0, 1):
        piece_in(0, 1, 2, half)
        across(0, 1, 2, half)
    peer_in(1, 1)
    multiply(1, 1, False)
    peer_in(0, 1)
    multiply(0, 1, False)

    ids = ids_ref[...]

    def turn_student(j, carry):
        top, hit = carry
        at = pl.ds(pl.multiple_of(j * 128, 128), 128)
        block = acc[:, at].T
        lt[at, :] = block
        column = lax.broadcasted_iota(jnp.int32, (128, 128), 0) + (v * VT + j * 128)
        found = jnp.where(column == ids, block, 0.0)
        return (
            jnp.maximum(top, block.reshape(16, 8, 128).max(axis=0)),
            hit + found.reshape(16, 8, 128).sum(axis=0),
        )

    zero8 = jnp.zeros((8, 128), F32)
    top, hit = lax.fori_loop(0, NT, turn_student, (jnp.full((8, 128), -jnp.inf, F32), zero8))
    s_max = top.max(axis=0, keepdims=True)

    def exp_student(j, carry):
        total, cross = carry
        at = pl.ds(pl.multiple_of(j * 128, 128), 128)
        s = lt[at, :]
        e = jnp.exp(s - s_max)
        x = et[at, :] * (tt[at, :] - s)
        lt[at, :] = e
        return total + e.reshape(16, 8, 128).sum(axis=0), cross + x.reshape(16, 8, 128).sum(axis=0)

    total, cross = lax.fori_loop(0, NT, exp_student, (zero8, zero8))
    s_sum = total.sum(axis=0, keepdims=True)
    x_sum = cross.sum(axis=0, keepdims=True)
    s_hit = hit.sum(axis=0, keepdims=True)
    stat[v] = jnp.concatenate([t_max, s_max, t_sum, x_sum, s_sum, s_hit, s_hit, s_hit], axis=0)

    k = 0
    for offset in far + [0]:
        for other in (1, 0):
            if other or offset:
                to = dev(d, (xh ^ other) * NZ + (z + offset) % NZ)
                send(stat.at[v], stat.at[v], s_send.at[k], s_recv, to)
                k += 1
    arrived(mrow.at[pl.ds(0, 15)], m_recv)
    count_row = mrow[0]
    for r in range(1, 16):
        count_row = count_row + mrow[r]
    count = jnp.sum(count_row, axis=1, keepdims=True)
    factor = mask_ref[...].astype(F32) / count
    arrived(stat.at[pl.ds(0, 31)], s_recv)
    tops = stat[0]
    for r in range(1, 32):
        tops = jnp.maximum(tops, stat[r])
    tops = tops[0:2]
    tz = xz = sz = hz = jnp.zeros((1, 128), F32)
    for r in range(32):
        one = stat[r]
        scale = jnp.exp(one[0:2] - tops)
        tz = tz + scale[0:1] * one[2:3]
        xz = xz + scale[0:1] * one[3:4]
        sz = sz + scale[1:2] * one[4:5]
        hz = hz + one[5:6]
    t_lse = tops[0:1] + jnp.log(tz)
    s_lse = tops[1:2] + jnp.log(sz)
    kl = xz / tz - t_lse + s_lse
    kl_ref[...] = kl
    samp_ref[...] = hz - s_lse
    lrow[d] = kl * mask_ref[...].astype(F32)
    for r in range(1, 16):
        send(lrow.at[d], lrow.at[d], l_send.at[r - 1], l_recv, dev(d ^ r, v))

    s_scale = factor * (jnp.exp(s_max - tops[1:2]) / sz)
    t_scale = factor * (jnp.exp(t_max - tops[0:1]) / tz)

    def make_dl(j, _):
        at = pl.ds(pl.multiple_of(j * 128, 128), 128)
        dl[at, :] = (lt[at, :] * s_scale - et[at, :] * t_scale).astype(BF16)
        return 0

    lax.fori_loop(0, NT, make_dl, 0)

    def quarter(half, q):
        rows = pl.ds(pl.multiple_of(half * 1024 + q * 256, 256), 256)
        return jnp.dot(w[rows, :], dl[...], preferred_element_type=F32)

    order = [(z // 4 + s) % 4 for s in (2, 1, 3, 0)]
    for i in range(4):
        xsend[i] = quarter(1 - xh, order[i]).astype(BF16)
        send(xsend.at[i], xrecv.at[i], x_send.at[i], x_recv.at[i], dev(d, v ^ NZ))
    for i in range(4):
        own[i] = quarter(xh, order[i])
    k = 0
    for i in range(4):
        arrived(xrecv.at[i], x_recv.at[i])
        both = own[i] + xrecv[i].astype(F32)
        own[i] = both
        zsend[i] = both.astype(BF16)
        for r in range(4) if i < 3 else (2, 3, 1):
            zt = order[i] * 4 + r if i < 3 else z ^ r
            piece = zsend.at[i, pl.ds(pl.multiple_of((zt % 4) * R, R), R)]
            send(piece, zrecv.at[z], z_send.at[k], z_recv, dev(d, xh * NZ + zt))
            k += 1

    arrived(lrow.at[pl.ds(0, 15)], l_recv)
    loss_row = lrow[0]
    for r in range(1, 16):
        loss_row = loss_row + lrow[r]
    loss_ref[...] = jnp.sum(loss_row, axis=1, keepdims=True) / count

    kept = own[3, pl.ds(pl.multiple_of((z % 4) * R, R), R), :]
    arrived(zrecv.at[pl.ds(0, 15)], z_recv)
    for r in range(1, 16):
        kept = kept + zrecv[z ^ r].astype(F32)
    turned = jnp.concatenate([kept, jnp.zeros((128 - R, TOK), F32)], axis=0).T
    grad_ref[...] = turned[:, :R].astype(BF16)
    for copy in started:
        copy.wait_send()


def on_device(hidden, blocks, teacher, ids, mask):
    vm = pl.BlockSpec(memory_space=pltpu.VMEM)
    dma = pltpu.SemaphoreType.DMA
    outs = pl.pallas_call(
        kernel,
        out_shape=(
            jax.ShapeDtypeStruct((TOK, R), BF16),
            jax.ShapeDtypeStruct((1, TOK), F32),
            jax.ShapeDtypeStruct((1, TOK), F32),
            jax.ShapeDtypeStruct((1, 1), F32),
        ),
        in_specs=[vm, pl.BlockSpec(memory_space=pl.ANY), vm, vm, vm],
        out_specs=(vm, vm, vm, vm),
        scratch_shapes=[
            pltpu.VMEM((D, VT), BF16),
            pltpu.VMEM((NZ, 2 * R, TOK), BF16),
            pltpu.VMEM((4, TOK, 512), BF16),
            pltpu.VMEM((TOK, VT), F32),
            pltpu.VMEM((VT, TOK), F32),
            pltpu.VMEM((VT, TOK), F32),
            pltpu.VMEM((VT, TOK), F32),
            pltpu.VMEM((VT, TOK), BF16),
            pltpu.VMEM((32, 8, TOK), F32),
            pltpu.VMEM((16, 1, TOK), F32),
            pltpu.VMEM((16, 1, TOK), F32),
            pltpu.VMEM((4, 256, TOK), BF16),
            pltpu.VMEM((4, 256, TOK), BF16),
            pltpu.VMEM((4, 256, TOK), F32),
            pltpu.VMEM((4, 256, TOK), BF16),
            pltpu.VMEM((NZ, R, TOK), BF16),
            dma((20,)), dma((20,)), dma((20,)), dma((20,)), dma, dma((16,)), dma((2,)),
            dma((31,)), dma, dma((15,)), dma, dma((15,)), dma, dma((4,)), dma((4,)), dma((15,)), dma,
        ],
        compiler_params=pltpu.CompilerParams(
            collective_id=0, has_side_effects=True, vmem_limit_bytes=60 * 1024 * 1024
        ),
    )(hidden, blocks.reshape(R, 2 * VT), teacher, ids.reshape(1, TOK), mask.reshape(1, TOK))
    return outs[0], outs[1].reshape(TOK), outs[2].reshape(TOK), outs[3].reshape(())


def solution(mesh):
    return jax.shard_map(
        on_device,
        mesh=mesh,
        in_specs=(P("dp", "vocab"), P("vocab", "dp", None), P("dp", "vocab"), P("dp"), P("dp")),
        out_specs=(P("dp", "vocab"), P("dp"), P("dp"), P()),
        check_vma=False,
    )
```

time: 264 us -> 106 us (0.40)
  the two profiles are of different devices: /device:TPU:34 before, /device:TPU:1 now
where the time goes in v1:
time: 106 us
  Pallas kernels  98.4 us (93%)
  local copies, waits for them, and re-layouts  4.66 us (4%)
  between operations  2.45 us (2%)
    pallas_call x1, Pallas kernels, on_device(): pl.pallas_call(kernel, out_shape=(jax.ShapeDtypeStruct((TOK, R), BF16), j...  98.4 us
    unnamed x8, local copies, waits for them, and re-layouts  4.66 us

profile of v1, /device:TPU:1, one launch (start us, length us, event | category | flops | bytes accessed | tf_op | source)
XLA Modules:
  0.0 105.5 jit_solution(18030148093463280423)
XLA Ops:
  0.6 1.4 %copy.9.hid_ref = bf16[128,64]{1,0:T(8,128)(2,1)} copy(bf16[128,64]{0,1:T(8,128)(2,1)} %param.5) | data formatting | bytes 32768 | tf_op args[0]
  2.1 98.4 %shard_map.84 = (bf16[128,64]{1,0:T(8,128)(2,1)}, f32[1,128]{1,0:T(1,128)}, f32[1,128]{1,0:T(1,128)}, f32[1,1]{1,0:T(1,128)}) custom-call(bf16[128,64]{1,0:T(8,128)(2,1)} %copy.9.hid_ref, bf16[64,4864]{1,0:T(8,128)(2,1)} %bitcast.6, bf16[128,2432]{1,0:T(8,128)(2,1)} %tea_ref.1, s32[1,128]{1,0:T(1,128)} %bitcast.7, s32[1,128]{1,0:T(1,128)} %bitcast.8), custom_call_target="tpu_custom_call" | custom-call | tf_op jit(solution)/shard_map/pallas_call | solution.py:331
  100.5 1.4 %copy.10 = bf16[128,64]{0,1:T(8,128)(2,1)} copy(bf16[128,64]{1,0:T(8,128)(2,1)} %get-tuple-element.12) | data formatting | bytes 32768
  101.9 0.0 copy-start.1
  101.9 0.7 copy-done.1
  102.6 0.0 copy-start
  102.6 0.5 copy.14
  103.1 0.1 copy-done
  103.2 0.5 copy.15
Async XLA Ops:
  101.9 0.7 copy-start.1
  102.6 0.6 copy-start

commit v2 on v1

v2 whole, which is shorter than its diff:
```python
import jax
import jax.numpy as jnp
from jax import lax
from jax.experimental import pallas as pl
from jax.experimental.pallas import tpu as pltpu
from jax.sharding import PartitionSpec as P

F32 = jnp.float32
BF16 = jnp.bfloat16
D = 2048
VT = 2432
TOK = 128
R = 64
NT = VT // 128
NZ = 16
MESH = pl.DeviceIdType.MESH

XP, YP, YM, ZP, CP = range(5)


def kernel(
    hid_hbm, blk_ref, tea_hbm, ids_hbm, mask_hbm,
    grad_ref, row_ref,
    w, ht, hg, acc, lt, tt, et, dl, stat, mrun, mgot, lrun, lgot, xsend, xrecv, own, zsend, zrecv,
    tea_ref, ids_ref, mask_ref,
    w_send, w_recv, d_send, d_recv, loc_sem, h_send, h_recv,
    s_send, s_recv, m_send, m_recv, l_send, l_recv, x_send, x_recv, z_send, z_recv, ready,
):
    d = lax.axis_index("dp")
    v = lax.axis_index("vocab")
    xl, y, c = d // 8, (d // 2) % 4, d % 2
    xh, z = v // NZ, v % NZ
    h = v % 2

    def dev(dp, vocab):
        return {"dp": dp, "vocab": vocab}

    def along_z(k):
        return dev(d, xh * NZ + (z + k) % NZ)

    target = {
        XP: dev(d ^ 8, v),
        YP: dev(xl * 8 + ((y + 1) % 4) * 2 + c, v),
        YM: dev(xl * 8 + ((y + 3) % 4) * 2 + c, v),
        ZP: dev(d, v ^ 1),
        CP: dev(d ^ 1, v),
    }
    across_x = dev(d, v ^ NZ)
    ladder = [target[CP], target[XP], dev(xl * 8 + (y ^ 1) * 2 + c, v), dev(xl * 8 + (3 - y) * 2 + c, v)]
    far = [8, 7, 9, 6, 10, 5, 11, 4, 12, 3, 13, 2, 14, 1, 15]
    mine = pl.ds(pl.multiple_of(xh * R, R), R)
    theirs = pl.ds(pl.multiple_of((1 - xh) * R, R), R)

    barrier = pltpu.get_barrier_semaphore()
    for to in (target[YP], target[YM], target[XP], target[CP], along_z(1), along_z(15), across_x):
        pl.semaphore_signal(barrier, inc=1, device_id=to, device_id_type=MESH)
    near = blk_ref.at[:, pl.ds(pl.multiple_of(h * VT, 128), VT)]
    away = blk_ref.at[:, pl.ds(pl.multiple_of((1 - h) * VT, 128), VT)]
    own_rows = pl.ds(pl.multiple_of(h * 1024 + R * d, R), R)
    fetches = [
        pltpu.make_async_copy(src, dst, loc_sem.at[i])
        for i, (src, dst) in enumerate(
            [
                (hid_hbm, ht.at[z, mine]),
                (mask_hbm, mask_ref),
                (tea_hbm, tea_ref),
                (ids_hbm, ids_ref),
                (near, w.at[own_rows]),
            ]
        )
    ]
    for fetch in fetches:
        fetch.start()
    fetches[0].wait()
    fetches[1].wait()
    mrun[0] = mask_ref[...].astype(F32)
    pl.semaphore_wait(barrier, 7)

    started = []

    def send(src, dst, ssem, rsem, to):
        copy = pltpu.make_async_remote_copy(
            src_ref=src, dst_ref=dst, send_sem=ssem, recv_sem=rsem, device_id=to, device_id_type=MESH
        )
        copy.start()
        started.append(copy)

    def arrived(dst, sem):
        pltpu.make_async_copy(dst, dst, sem).wait()

    def tell(i, *to):
        for device in to:
            pl.semaphore_signal(ready.at[i], inc=1, device_id=device, device_id_type=MESH)

    def climb(run, got, ssem, rsem, step):
        if step:
            arrived(got.at[step - 1], rsem.at[step - 1])
            run[step] = run[step - 1] + got[step - 1]
        if step < 4:
            send(run.at[step], got.at[step], ssem.at[step], rsem.at[step], ladder[step])

    def rows_of(u, dx, dy, core, sub=None):
        base = (h ^ (u // 2)) * 1024 + R * ((xl ^ dx) * 8 + ((y + dy) % 4) * 2 + core) + 32 * (u % 2)
        if sub is None:
            return pl.ds(pl.multiple_of(base, 32), 32)
        return pl.ds(pl.multiple_of(base + 16 * sub, 16), 16)

    counter = {"w": 0, "d": 0}
    subs = {(0, 1, 1, 0): 32, (0, 1, 3, 1): 33, (0, 1, 1, 1): None, (0, 1, 3, 0): None}

    def sem_of(u, dx, dy, sub=None):
        return subs.get((u, dx, dy, sub)) or u * 8 + dx * 4 + dy

    def pass_on(u, dx, dy, way, sub=None, src=None):
        ref = w.at[rows_of(u, dx, dy, c, sub)]
        if way == XP:
            at = (u, dx ^ 1, dy, sub)
        elif way == YP:
            at = (u, dx, (dy + 3) % 4, sub)
        elif way == YM:
            at = (u, dx, (dy + 1) % 4, sub)
        k = counter["w"]
        counter["w"] += 1
        send(ref if src is None else src, ref, w_send.at[k], w_recv.at[sem_of(*at)], target[way])

    def across(u, dx, dy):
        ref = w.at[rows_of(u, dx, dy, c)]
        k = counter["d"]
        counter["d"] += 1
        send(ref, ref, d_send.at[k], d_recv.at[sem_of(u, dx, dy)], target[CP])

    def piece_in(u, dx, dy, sub=None):
        arrived(w.at[rows_of(u, dx, dy, c, sub)], w_recv.at[sem_of(u, dx, dy, sub)])

    def peer_in(t, dx):
        for u in (2 * t, 2 * t + 1):
            for dy in range(4):
                if (u, dx, dy) != (1, 0, 0) and (u, dx, dy) != (0, 0, 0):
                    arrived(w.at[rows_of(u, dx, dy, 1 - c)], d_recv.at[sem_of(u, dx, dy)])

    for u in (0, 1):
        lines = pl.ds(32 * u, 32)
        for way in (XP, YP, YM):
            pass_on(u, 0, 0, way, src=near.at[lines])
        there = pl.ds(pl.multiple_of(h * 1024 + R * d + 32 * u, 32), 32)
        send(away.at[lines], w.at[there], w_send.at[46 + u], w_recv.at[sem_of(2 + u, 0, 0)], target[ZP])
    send(ht.at[z, mine], ht.at[z, mine], h_send.at[15], h_recv.at[1], across_x)
    send(near, w.at[own_rows], d_send.at[31], d_recv.at[0], target[CP])
    tell(0, along_z(1), along_z(15))
    climb(mrun, mgot, m_send, m_recv, 0)

    def turn_teacher(j, top):
        at = pl.ds(pl.multiple_of(j * 128, 128), 128)
        block = tea_ref[:, at].astype(F32).T
        tt[at, :] = block
        return jnp.maximum(top, block.reshape(16, 8, 128).max(axis=0))

    fetches[2].wait()
    top = lax.fori_loop(0, NT, turn_teacher, jnp.full((8, 128), -jnp.inf, F32))
    t_max = top.max(axis=0, keepdims=True)
    pl.semaphore_wait(ready.at[0], 2)
    tell(1, along_z(2), along_z(14))

    def exp_teacher(j, total):
        at = pl.ds(pl.multiple_of(j * 128, 128), 128)
        e = jnp.exp(tt[at, :] - t_max)
        et[at, :] = e
        return total + e.reshape(16, 8, 128).sum(axis=0)

    t_sum = lax.fori_loop(0, NT, exp_teacher, jnp.zeros((8, 128), F32)).sum(axis=0, keepdims=True)
    climb(mrun, mgot, m_send, m_recv, 1)

    hidden = iter(range(15))

    def spread(*steps):
        for k in steps:
            send(ht.at[z], ht.at[z], h_send.at[next(hidden)], h_recv.at[0], along_z(k))

    arrived(ht.at[z, theirs], h_recv.at[1])
    spread(1, 15, 2, 14)
    pl.semaphore_wait(ready.at[1], 2)
    tell(2, along_z(4), along_z(12))
    spread(3, 13, 4, 12)

    piece_in(0, 0, 3)
    pass_on(0, 0, 3, YP)
    across(0, 0, 3)
    piece_in(0, 0, 1)
    across(0, 0, 1)
    piece_in(2, 0, 0)
    pass_on(2, 0, 0, XP)
    pass_on(2, 0, 0, YP)
    pass_on(2, 0, 0, YM)
    pass_on(0, 0, 3, XP, sub=1)
    pass_on(0, 0, 1, XP, sub=0)
    across(2, 0, 0)
    piece_in(0, 1, 0)
    across(0, 1, 0)
    climb(mrun, mgot, m_send, m_recv, 2)
    piece_in(1, 0, 1)
    pass_on(1, 0, 1, YM)
    across(1, 0, 1)
    piece_in(1, 0, 3)
    across(1, 0, 3)
    piece_in(3, 0, 0)
    pass_on(3, 0, 0, YP)
    pass_on(3, 0, 0, YM)
    pass_on(3, 0, 0, XP)
    across(3, 0, 0)
    piece_in(1, 1, 0)
    across(1, 1, 0)
    pl.semaphore_wait(ready.at[2], 2)
    tell(3, across_x)
    spread(8, 7, 9, 6, 10, 5, 11)
    piece_in(0, 0, 2)
    pass_on(0, 0, 2, XP)
    across(0, 0, 2)
    piece_in(2, 0, 1)
    across(2, 0, 1)
    piece_in(2, 1, 0)
    across(2, 1, 0)
    climb(mrun, mgot, m_send, m_recv, 3)
    piece_in(2, 0, 3)
    pass_on(2, 0, 3, YP)
    across(2, 0, 3)
    piece_in(1, 0, 2)
    pass_on(1, 0, 2, XP)
    across(1, 0, 2)
    piece_in(3, 0, 1)
    pass_on(3, 0, 1, YM)
    across(3, 0, 1)
    for u in (0, 1, 2):
        pass_on(u, 1, 0, YP, sub=None if u else 0)
        pass_on(u, 1, 0, YM, sub=None if u else 1)
    piece_in(3, 0, 3)
    across(3, 0, 3)
    piece_in(3, 1, 0)
    pass_on(3, 1, 0, YP)
    pass_on(3, 1, 0, YM)
    across(3, 1, 0)
    piece_in(2, 0, 2)
    pass_on(2, 0, 2, XP)
    across(2, 0, 2)
    piece_in(3, 0, 2)
    pass_on(3, 0, 2, XP)
    across(3, 0, 2)
    piece_in(0, 1, 2)
    across(0, 1, 2)
    climb(mrun, mgot, m_send, m_recv, 4)

    arrived(ht.at[pl.ds(0, 15)], h_recv.at[0])
    for g in range(4):
        part = ht[8 * (g % 2) : 8 * (g % 2) + 8, (g // 2) * R : (g // 2) * R + R, :]
        hg[g] = part.reshape(512, TOK).astype(F32).T.astype(BF16)

    def multiply(t, dx, first):
        g = (h ^ t) * 2 + (xl ^ dx)
        rows = pl.ds(pl.multiple_of(g * 512, 512), 512)
        part = jnp.dot(hg[g], w[rows, :], preferred_element_type=F32)
        acc[...] = part if first else acc[...] + part

    fetches[4].wait()
    other_rows = pl.ds(pl.multiple_of(h * 1024 + R * (d ^ 1), R), R)
    arrived(w.at[other_rows], d_recv.at[0])
    peer_in(0, 0)
    multiply(0, 0, True)
    for dy in (3, 1):
        for sub in (0, 1):
            piece_in(0, 1, dy, sub)
        across(0, 1, dy)
    for dy in (2, 3, 1):
        piece_in(1, 1, dy)
        across(1, 1, dy)
    peer_in(1, 0)
    multiply(1, 0, False)
    for u in (2, 3):
        for dy in (2, 3, 1):
            piece_in(u, 1, dy)
            across(u, 1, dy)
        if u == 2:
            peer_in(0, 1)
            multiply(0, 1, False)
    peer_in(1, 1)
    multiply(1, 1, False)
    pl.semaphore_wait(ready.at[3], 1)
    fetches[3].wait()

    ids = ids_ref[...]

    def turn_student(j, carry):
        top, hit = carry
        at = pl.ds(pl.multiple_of(j * 128, 128), 128)
        block = acc[:, at].T
        lt[at, :] = block
        column = lax.broadcasted_iota(jnp.int32, (128, 128), 0) + (v * VT + j * 128)
        found = jnp.where(column == ids, block, 0.0)
        return (
            jnp.maximum(top, block.reshape(16, 8, 128).max(axis=0)),
            hit + found.reshape(16, 8, 128).sum(axis=0),
        )

    zero8 = jnp.zeros((8, 128), F32)
    top, hit = lax.fori_loop(0, NT, turn_student, (jnp.full((8, 128), -jnp.inf, F32), zero8))
    s_max = top.max(axis=0, keepdims=True)

    def exp_student(j, carry):
        total, cross = carry
        at = pl.ds(pl.multiple_of(j * 128, 128), 128)
        s = lt[at, :]
        e = jnp.exp(s - s_max)
        x = et[at, :] * (tt[at, :] - s)
        lt[at, :] = e
        return total + e.reshape(16, 8, 128).sum(axis=0), cross + x.reshape(16, 8, 128).sum(axis=0)

    total, cross = lax.fori_loop(0, NT, exp_student, (zero8, zero8))
    s_sum = total.sum(axis=0, keepdims=True)
    x_sum = cross.sum(axis=0, keepdims=True)
    s_hit = hit.sum(axis=0, keepdims=True)
    stat[v] = jnp.concatenate([t_max, s_max, t_sum, x_sum, s_sum, s_hit, s_hit, s_hit], axis=0)

    k = 0
    for offset in far + [0]:
        for other in (1, 0):
            if other or offset:
                to = dev(d, (xh ^ other) * NZ + (z + offset) % NZ)
                send(stat.at[v], stat.at[v], s_send.at[k], s_recv, to)
                k += 1
    count = jnp.sum(mrun[4], axis=1, keepdims=True)
    factor = mask_ref[...].astype(F32) / count
    arrived(stat.at[pl.ds(0, 31)], s_recv)
    tops = stat[0]
    for r in range(1, 32):
        tops = jnp.maximum(tops, stat[r])
    tops = tops[0:2]
    tz = xz = sz = hz = jnp.zeros((1, 128), F32)
    for r in range(32):
        one = stat[r]
        scale = jnp.exp(one[0:2] - tops)
        tz = tz + scale[0:1] * one[2:3]
        xz = xz + scale[0:1] * one[3:4]
        sz = sz + scale[1:2] * one[4:5]
        hz = hz + one[5:6]
    t_lse = tops[0:1] + jnp.log(tz)
    s_lse = tops[1:2] + jnp.log(sz)
    kl = xz / tz - t_lse + s_lse
    row_ref[0:1] = kl
    row_ref[1:2] = hz - s_lse
    lrun[0] = kl * mask_ref[...].astype(F32)
    climb(lrun, lgot, l_send, l_recv, 0)

    s_scale = factor * (jnp.exp(s_max - tops[1:2]) / sz)
    t_scale = factor * (jnp.exp(t_max - tops[0:1]) / tz)

    def make_dl(j, _):
        at = pl.ds(pl.multiple_of(j * 128, 128), 128)
        dl[at, :] = (lt[at, :] * s_scale - et[at, :] * t_scale).astype(BF16)
        return 0

    lax.fori_loop(0, NT, make_dl, 0)

    def quarter(half, q):
        rows = pl.ds(pl.multiple_of(half * 1024 + q * 256, 256), 256)
        return jnp.dot(w[rows, :], dl[...], preferred_element_type=F32)

    order = (0, 1, 3, 2)
    for step, q in enumerate(order):
        xsend[q] = quarter(1 - xh, q).astype(BF16)
        send(xsend.at[q], xrecv.at[q], x_send.at[q], x_recv.at[q], across_x)
    climb(lrun, lgot, l_send, l_recv, 1)
    for q in order:
        own[q] = quarter(xh, q)
    climb(lrun, lgot, l_send, l_recv, 2)
    elsewhere = []
    for q in order:
        arrived(xrecv.at[q], x_recv.at[q])
        both = own[q] + xrecv[q].astype(F32)
        own[q] = both
        zsend[q] = both.astype(BF16)
        for r in range(4):
            zt = q * 4 + r
            copy = pltpu.make_async_remote_copy(
                src_ref=zsend.at[q, pl.ds(r * R, R)],
                dst_ref=zrecv.at[z],
                send_sem=z_send.at[zt],
                recv_sem=z_recv,
                device_id=dev(d, xh * NZ + zt),
                device_id_type=MESH,
            )
            pl.when(z != zt)(copy.start)
            elsewhere.append((zt, copy))

    climb(lrun, lgot, l_send, l_recv, 3)
    climb(lrun, lgot, l_send, l_recv, 4)
    loss = jnp.sum(lrun[4], axis=1, keepdims=True) / count
    row_ref[2:3] = jnp.broadcast_to(loss, (1, TOK))

    kept = own[z // 4, pl.ds(pl.multiple_of((z % 4) * R, R), R), :]
    arrived(zrecv.at[pl.ds(0, 15)], z_recv)
    for r in range(1, 16):
        kept = kept + zrecv[z ^ r].astype(F32)
    grad_ref[...] = kept.astype(BF16)
    for zt, copy in elsewhere:
        pl.when(z != zt)(copy.wait_send)
    for copy in started:
        copy.wait_send()


def place(grad_in, row_in, grad_ref, kl_ref, samp_ref, loss_ref):
    grad_ref[...] = grad_in[...]
    kl_ref[...] = row_in[0]
    samp_ref[...] = row_in[1]
    loss_ref[...] = row_in[2:3, 0:1]


def on_device(hidden, blocks, teacher, ids, mask):
    vm = pl.BlockSpec(memory_space=pltpu.VMEM)
    hbm = pl.BlockSpec(memory_space=pl.ANY)
    dma = pltpu.SemaphoreType.DMA
    grad, rows = pl.pallas_call(
        kernel,
        out_shape=(jax.ShapeDtypeStruct((R, TOK), BF16), jax.ShapeDtypeStruct((8, TOK), F32)),
        in_specs=[hbm] * 5,
        out_specs=(vm, vm),
        scratch_shapes=[
            pltpu.VMEM((D, VT), BF16),
            pltpu.VMEM((NZ, 2 * R, TOK), BF16),
            pltpu.VMEM((4, TOK, 512), BF16),
            pltpu.VMEM((TOK, VT), F32),
            pltpu.VMEM((VT, TOK), F32),
            pltpu.VMEM((VT, TOK), F32),
            pltpu.VMEM((VT, TOK), F32),
            pltpu.VMEM((VT, TOK), BF16),
            pltpu.VMEM((32, 8, TOK), F32),
            pltpu.VMEM((5, 1, TOK), F32),
            pltpu.VMEM((4, 1, TOK), F32),
            pltpu.VMEM((5, 1, TOK), F32),
            pltpu.VMEM((4, 1, TOK), F32),
            pltpu.VMEM((4, 256, TOK), BF16),
            pltpu.VMEM((4, 256, TOK), BF16),
            pltpu.VMEM((4, 256, TOK), F32),
            pltpu.VMEM((4, 256, TOK), BF16),
            pltpu.VMEM((NZ, R, TOK), BF16),
            pltpu.VMEM((TOK, VT), BF16),
            pltpu.VMEM((1, TOK), jnp.int32),
            pltpu.VMEM((1, TOK), jnp.int32),
            dma((48,)), dma((34,)), dma((32,)), dma((32,)), dma((5,)), dma((16,)), dma((2,)),
            dma((31,)), dma, dma((4,)), dma((4,)), dma((4,)), dma((4,)), dma((4,)), dma((4,)), dma((16,)), dma,
            pltpu.SemaphoreType.REGULAR((4,)),
        ],
        compiler_params=pltpu.CompilerParams(
            collective_id=0, has_side_effects=True, vmem_limit_bytes=60 * 1024 * 1024
        ),
    )(hidden.T, blocks.reshape(R, 2 * VT), teacher, ids.reshape(1, TOK), mask.reshape(1, TOK))
    grad, kl, samp, loss = pl.pallas_call(
        place,
        out_shape=(
            jax.ShapeDtypeStruct((R, TOK), BF16),
            jax.ShapeDtypeStruct((TOK,), F32),
            jax.ShapeDtypeStruct((TOK,), F32),
            jax.ShapeDtypeStruct((1, 1), F32),
        ),
        in_specs=[vm, vm],
        out_specs=(vm, vm, vm, vm),
    )(grad, rows)
    return grad.T, kl, samp, loss.reshape(())


def solution(mesh):
    return jax.shard_map(
        on_device,
        mesh=mesh,
        in_specs=(P("dp", "vocab"), P("vocab", "dp", None), P("dp", "vocab"), P("dp"), P("dp")),
        out_specs=(P("dp", "vocab"), P("dp"), P("dp"), P()),
        check_vma=False,
    )
```

time: 106 us -> 88.9 us (0.84)
  the two profiles are of different devices: /device:TPU:1 before, /device:TPU:66 now
where the time goes in v2:
time: 88.9 us; the launch traced here: 88.6 us
  Pallas kernels  88 us (99%)
    pallas_call x1, Pallas kernels, on_device(): pl.pallas_call(kernel, out_shape=(jax.ShapeDtypeStruct((R, TOK), BF16), j...  86.6 us

profile of v2, /device:TPU:66, one launch (start us, length us, event | category | flops | bytes accessed | tf_op | source)
XLA Modules:
  0.0 88.6 jit_solution(574594543980372799)
XLA Ops:
  0.6 86.6 %shard_map.84 = (bf16[64,128]{1,0:T(8,128)(2,1)}, f32[8,128]{1,0:T(8,128)}) custom-call(bf16[64,128]{1,0:T(8,128)(2,1)} %bitcast.7, bf16[64,4864]{1,0:T(8,128)(2,1)} %bitcast.6, bf16[128,2432]{1,0:T(8,128)(2,1)} %tea_hbm.1, s32[1,128]{1,0:T(1,128)} %bitcast.8, s32[1,128]{1,0:T(1,128)} %bitcast.9), custom_call_target="tpu_custom_call" | custom-call | tf_op jit(solution)/shard_map/pallas_call | solution.py:419
  87.3 1.3 %shard_map.85 = (bf16[64,128]{1,0:T(8,128)(2,1)}, f32[128]{0:T(128)}, f32[128]{0:T(128)}, f32[1,1]{1,0:T(1,128)}) custom-call(bf16[64,128]{1,0:T(8,128)(2,1)} %get-tuple-element.10.grad_in, f32[8,128]{1,0:T(8,128)} %get-tuple-element.11.row_in), custom_call_target="tpu_custom_call" | custom-call | tf_op jit(solution)/shard_map/pallas_call | solution.py:454

commit v3 on v2

--- a/solution.py
+++ b/solution.py
@@ -12,6 +12,9 @@
 TOK = 128
 R = 64
 NT = VT // 128
+CUT = 1280
+COLS = (pl.ds(0, CUT), pl.ds(CUT, VT - CUT))
+TILES = (range(CUT // 128), range(CUT // 128, NT))
 NZ = 16
 MESH = pl.DeviceIdType.MESH
 
@@ -99,11 +102,11 @@
         if step < 4:
             send(run.at[step], got.at[step], ssem.at[step], rsem.at[step], ladder[step])
 
-    def rows_of(u, dx, dy, core, sub=None):
-        base = (h ^ (u // 2)) * 1024 + R * ((xl ^ dx) * 8 + ((y + dy) % 4) * 2 + core) + 32 * (u % 2)
+    def unit(u, dx, dy, core, sub=None):
+        base = (h ^ (u // 2)) * 1024 + R * ((xl ^ dx) * 8 + ((y + dy) % 4) * 2 + core)
         if sub is None:
-            return pl.ds(pl.multiple_of(base, 32), 32)
-        return pl.ds(pl.multiple_of(base + 16 * sub, 16), 16)
+            return w.at[pl.ds(pl.multiple_of(base, R), R), COLS[u % 2]]
+        return w.at[pl.ds(pl.multiple_of(base + 32 * sub, 32), 32), COLS[u % 2]]
 
     counter = {"w": 0, "d": 0}
     subs = {(0, 1, 1, 0): 32, (0, 1, 3, 1): 33, (0, 1, 1, 1): None, (0, 1, 3, 0): None}
@@ -112,7 +115,7 @@
         return subs.get((u, dx, dy, sub)) or u * 8 + dx * 4 + dy
 
     def pass_on(u, dx, dy, way, sub=None, src=None):
-        ref = w.at[rows_of(u, dx, dy, c, sub)]
+        ref = unit(u, dx, dy, c, sub)
         if way == XP:
             at = (u, dx ^ 1, dy, sub)
         elif way == YP:
@@ -124,63 +127,66 @@
         send(ref if src is None else src, ref, w_send.at[k], w_recv.at[sem_of(*at)], target[way])
 
     def across(u, dx, dy):
-        ref = w.at[rows_of(u, dx, dy, c)]
+        ref = unit(u, dx, dy, c)
         k = counter["d"]
         counter["d"] += 1
         send(ref, ref, d_send.at[k], d_recv.at[sem_of(u, dx, dy)], target[CP])
 
     def piece_in(u, dx, dy, sub=None):
-        arrived(w.at[rows_of(u, dx, dy, c, sub)], w_recv.at[sem_of(u, dx, dy, sub)])
-
-    def peer_in(t, dx):
-        for u in (2 * t, 2 * t + 1):
-            for dy in range(4):
-                if (u, dx, dy) != (1, 0, 0) and (u, dx, dy) != (0, 0, 0):
-                    arrived(w.at[rows_of(u, dx, dy, 1 - c)], d_recv.at[sem_of(u, dx, dy)])
+        arrived(unit(u, dx, dy, c, sub), w_recv.at[sem_of(u, dx, dy, sub)])
+
+    def peer_in(u, dx):
+        for dy in range(4):
+            if (u, dx, dy) not in ((0, 0, 0), (1, 0, 0)):
+                arrived(unit(u, dx, dy, 1 - c), d_recv.at[sem_of(u, dx, dy)])
 
     for u in (0, 1):
-        lines = pl.ds(32 * u, 32)
         for way in (XP, YP, YM):
-            pass_on(u, 0, 0, way, src=near.at[lines])
-        there = pl.ds(pl.multiple_of(h * 1024 + R * d + 32 * u, 32), 32)
-        send(away.at[lines], w.at[there], w_send.at[46 + u], w_recv.at[sem_of(2 + u, 0, 0)], target[ZP])
+            pass_on(u, 0, 0, way, src=near.at[:, COLS[u]])
+        send(away.at[:, COLS[u]], w.at[own_rows, COLS[u]], w_send.at[46 + u], w_recv.at[sem_of(2 + u, 0, 0)], target[ZP])
     send(ht.at[z, mine], ht.at[z, mine], h_send.at[15], h_recv.at[1], across_x)
     send(near, w.at[own_rows], d_send.at[31], d_recv.at[0], target[CP])
     tell(0, along_z(1), along_z(15))
     climb(mrun, mgot, m_send, m_recv, 0)
 
-    def turn_teacher(j, top):
-        at = pl.ds(pl.multiple_of(j * 128, 128), 128)
-        block = tea_ref[:, at].astype(F32).T
-        tt[at, :] = block
-        return jnp.maximum(top, block.reshape(16, 8, 128).max(axis=0))
-
     fetches[2].wait()
-    top = lax.fori_loop(0, NT, turn_teacher, jnp.full((8, 128), -jnp.inf, F32))
+    def fold(block, how):
+        return how(block.reshape(16, 8, 128), axis=0)
+
+    def tile(j):
+        return slice(j * 128, j * 128 + 128)
+
+    low8 = jnp.full((8, 128), -jnp.inf, F32)
+    zero8 = jnp.zeros((8, 128), F32)
+    top = low8
+    for j in range(NT):
+        block = tea_ref[:, tile(j)].astype(F32).T
+        tt[tile(j), :] = block
+        top = jnp.maximum(top, fold(block, jnp.max))
     t_max = top.max(axis=0, keepdims=True)
     pl.semaphore_wait(ready.at[0], 2)
     tell(1, along_z(2), along_z(14))
 
-    def exp_teacher(j, total):
-        at = pl.ds(pl.multiple_of(j * 128, 128), 128)
-        e = jnp.exp(tt[at, :] - t_max)
-        et[at, :] = e
-        return total + e.reshape(16, 8, 128).sum(axis=0)
-
-    t_sum = lax.fori_loop(0, NT, exp_teacher, jnp.zeros((8, 128), F32)).sum(axis=0, keepdims=True)
+    total = zero8
+    for j in range(NT):
+        e = jnp.exp(tt[tile(j), :] - t_max)
+        et[tile(j), :] = e
+        total = total + fold(e, jnp.sum)
+    t_sum = total.sum(axis=0, keepdims=True)
     climb(mrun, mgot, m_send, m_recv, 1)
 
     hidden = iter(range(15))
 
-    def spread(*steps):
+    def spread(source, *steps):
         for k in steps:
-            send(ht.at[z], ht.at[z], h_send.at[next(hidden)], h_recv.at[0], along_z(k))
+            rsem = {4: 2, 12: 3}.get(k, 0) if source is z else 0
+            send(ht.at[source], ht.at[source], h_send.at[next(hidden)], h_recv.at[rsem], along_z(k))
 
     arrived(ht.at[z, theirs], h_recv.at[1])
-    spread(1, 15, 2, 14)
+    spread(z, 1, 15, 2, 14)
     pl.semaphore_wait(ready.at[1], 2)
     tell(2, along_z(4), along_z(12))
-    spread(3, 13, 4, 12)
+    spread(z, 3, 13, 4, 12)
 
     piece_in(0, 0, 3)
     pass_on(0, 0, 3, YP)
@@ -209,9 +215,6 @@
     across(3, 0, 0)
     piece_in(1, 1, 0)
     across(1, 1, 0)
-    pl.semaphore_wait(ready.at[2], 2)
-    tell(3, across_x)
-    spread(8, 7, 9, 6, 10, 5, 11)
     piece_in(0, 0, 2)
     pass_on(0, 0, 2, XP)
     across(0, 0, 2)
@@ -226,6 +229,11 @@
     piece_in(1, 0, 2)
     pass_on(1, 0, 2, XP)
     across(1, 0, 2)
+    before, after = (z + 12) % NZ, (z + 4) % NZ
+    arrived(ht.at[before], h_recv.at[2])
+    spread(before, 4, 3, 2, 1)
+    arrived(ht.at[after], h_recv.at[3])
+    spread(after, 13, 14, 15)
     piece_in(3, 0, 1)
     pass_on(3, 0, 1, YM)
     across(3, 0, 1)
@@ -248,74 +256,80 @@
     across(0, 1, 2)
     climb(mrun, mgot, m_send, m_recv, 4)
 
-    arrived(ht.at[pl.ds(0, 15)], h_recv.at[0])
+    pl.semaphore_wait(ready.at[2], 2)
+    tell(3, across_x)
+
+    arrived(ht.at[pl.ds(0, 13)], h_recv.at[0])
     for g in range(4):
         part = ht[8 * (g % 2) : 8 * (g % 2) + 8, (g // 2) * R : (g // 2) * R + R, :]
         hg[g] = part.reshape(512, TOK).astype(F32).T.astype(BF16)
 
-    def multiply(t, dx, first):
-        g = (h ^ t) * 2 + (xl ^ dx)
+    def multiply(u, dx):
+        g = (h ^ (u // 2)) * 2 + (xl ^ dx)
         rows = pl.ds(pl.multiple_of(g * 512, 512), 512)
-        part = jnp.dot(hg[g], w[rows, :], preferred_element_type=F32)
-        acc[...] = part if first else acc[...] + part
-
+        cols = COLS[u % 2]
+        part = jnp.dot(hg[g], w[rows, cols], preferred_element_type=F32)
+        acc[:, cols] = part if (u // 2, dx) == (0, 0) else acc[:, cols] + part
+
+    def statistics(p):
+        top, hit = low8, zero8
+        for j in TILES[p]:
+            block = acc[:, tile(j)].T
+            lt[tile(j), :] = block
+            column = lax.broadcasted_iota(jnp.int32, (128, 128), 0) + (v * VT + j * 128)
+            top = jnp.maximum(top, fold(block, jnp.max))
+            hit = hit + fold(jnp.where(column == ids, block, 0.0), jnp.sum)
+        high = top.max(axis=0, keepdims=True)
+        total, cross = zero8, zero8
+        for j in TILES[p]:
+            logit = lt[tile(j), :]
+            e = jnp.exp(logit - high)
+            lt[tile(j), :] = e
+            total = total + fold(e, jnp.sum)
+            cross = cross + fold(et[tile(j), :] * (tt[tile(j), :] - logit), jnp.sum)
+        return high, *(a.sum(axis=0, keepdims=True) for a in (total, cross, hit))
+
+    fetches[3].wait()
+    ids = ids_ref[...]
     fetches[4].wait()
     other_rows = pl.ds(pl.multiple_of(h * 1024 + R * (d ^ 1), R), R)
     arrived(w.at[other_rows], d_recv.at[0])
-    peer_in(0, 0)
-    multiply(0, 0, True)
+    for u in (0, 1):
+        peer_in(u, 0)
+        multiply(u, 0)
     for dy in (3, 1):
         for sub in (0, 1):
             piece_in(0, 1, dy, sub)
         across(0, 1, dy)
+    for u in (2, 3):
+        peer_in(u, 0)
+        multiply(u, 0)
     for dy in (2, 3, 1):
         piece_in(1, 1, dy)
         across(1, 1, dy)
-    peer_in(1, 0)
-    multiply(1, 0, False)
-    for u in (2, 3):
-        for dy in (2, 3, 1):
-            piece_in(u, 1, dy)
-            across(u, 1, dy)
-        if u == 2:
-            peer_in(0, 1)
-            multiply(0, 1, False)
+    peer_in(0, 1)
+    multiply(0, 1)
+    for dy in (2, 3, 1):
+        piece_in(2, 1, dy)
+        across(2, 1, dy)
     peer_in(1, 1)
-    multiply(1, 1, False)
+    multiply(1, 1)
+    peer_in(2, 1)
+    multiply(2, 1)
+    piece_in(3, 1, 2)
+    across(3, 1, 2)
+    max_0, sum_0, cross_0, hit_0 = statistics(0)
+    for dy in (3, 1):
+        piece_in(3, 1, dy)
+        across(3, 1, dy)
     pl.semaphore_wait(ready.at[3], 1)
-    fetches[3].wait()
-
-    ids = ids_ref[...]
-
-    def turn_student(j, carry):
-        top, hit = carry
-        at = pl.ds(pl.multiple_of(j * 128, 128), 128)
-        block = acc[:, at].T
-        lt[at, :] = block
-        column = lax.broadcasted_iota(jnp.int32, (128, 128), 0) + (v * VT + j * 128)
-        found = jnp.where(column == ids, block, 0.0)
-        return (
-            jnp.maximum(top, block.reshape(16, 8, 128).max(axis=0)),
-            hit + found.reshape(16, 8, 128).sum(axis=0),
-        )
-
-    zero8 = jnp.zeros((8, 128), F32)
-    top, hit = lax.fori_loop(0, NT, turn_student, (jnp.full((8, 128), -jnp.inf, F32), zero8))
-    s_max = top.max(axis=0, keepdims=True)
-
-    def exp_student(j, carry):
-        total, cross = carry
-        at = pl.ds(pl.multiple_of(j * 128, 128), 128)
-        s = lt[at, :]
-        e = jnp.exp(s - s_max)
-        x = et[at, :] * (tt[at, :] - s)
-        lt[at, :] = e
-        return total + e.reshape(16, 8, 128).sum(axis=0), cross + x.reshape(16, 8, 128).sum(axis=0)
-
-    total, cross = lax.fori_loop(0, NT, exp_student, (zero8, zero8))
-    s_sum = total.sum(axis=0, keepdims=True)
-    x_sum = cross.sum(axis=0, keepdims=True)
-    s_hit = hit.sum(axis=0, keepdims=True)
+    peer_in(3, 1)
+    multiply(3, 1)
+    max_1, sum_1, cross_1, hit_1 = statistics(1)
+    s_max = jnp.maximum(max_0, max_1)
+    s_sum = sum_0 * jnp.exp(max_0 - s_max) + sum_1 * jnp.exp(max_1 - s_max)
+    x_sum = cross_0 + cross_1
+    s_hit = hit_0 + hit_1
     stat[v] = jnp.concatenate([t_max, s_max, t_sum, x_sum, s_sum, s_hit, s_hit, s_hit], axis=0)
 
     k = 0
@@ -348,59 +362,48 @@
     lrun[0] = kl * mask_ref[...].astype(F32)
     climb(lrun, lgot, l_send, l_recv, 0)
 
-    s_scale = factor * (jnp.exp(s_max - tops[1:2]) / sz)
     t_scale = factor * (jnp.exp(t_max - tops[0:1]) / tz)
-
-    def make_dl(j, _):
-        at = pl.ds(pl.multiple_of(j * 128, 128), 128)
-        dl[at, :] = (lt[at, :] * s_scale - et[at, :] * t_scale).astype(BF16)
-        return 0
-
-    lax.fori_loop(0, NT, make_dl, 0)
+    for p, high in enumerate((max_0, max_1)):
+        s_scale = factor * (jnp.exp(high - tops[1:2]) / sz)
+        for j in TILES[p]:
+            dl[tile(j), :] = (lt[tile(j), :] * s_scale - et[tile(j), :] * t_scale).astype(BF16)
 
     def quarter(half, q):
         rows = pl.ds(pl.multiple_of(half * 1024 + q * 256, 256), 256)
         return jnp.dot(w[rows, :], dl[...], preferred_element_type=F32)
 
-    order = (0, 1, 3, 2)
-    for step, q in enumerate(order):
-        xsend[q] = quarter(1 - xh, q).astype(BF16)
-        send(xsend.at[q], xrecv.at[q], x_send.at[q], x_recv.at[q], across_x)
+    zq = z // 4
+    first, second = 2 * ((3 - zq) // 3), 3 - 2 * (zq // 2)
+    order = (first, second, 6 - first - second - zq, zq)
+    for i, q in enumerate(order):
+        xsend[i] = quarter(1 - xh, q).astype(BF16)
+        send(xsend.at[i], xrecv.at[i], x_send.at[i], x_recv.at[i], across_x)
     climb(lrun, lgot, l_send, l_recv, 1)
-    for q in order:
-        own[q] = quarter(xh, q)
+    for i, q in enumerate(order):
+        own[i] = quarter(xh, q)
     climb(lrun, lgot, l_send, l_recv, 2)
-    elsewhere = []
-    for q in order:
-        arrived(xrecv.at[q], x_recv.at[q])
-        both = own[q] + xrecv[q].astype(F32)
-        own[q] = both
-        zsend[q] = both.astype(BF16)
-        for r in range(4):
-            zt = q * 4 + r
-            copy = pltpu.make_async_remote_copy(
-                src_ref=zsend.at[q, pl.ds(r * R, R)],
-                dst_ref=zrecv.at[z],
-                send_sem=z_send.at[zt],
-                recv_sem=z_recv,
-                device_id=dev(d, xh * NZ + zt),
-                device_id_type=MESH,
-            )
-            pl.when(z != zt)(copy.start)
-            elsewhere.append((zt, copy))
+    k = 0
+    for i, q in enumerate(order):
+        arrived(xrecv.at[i], x_recv.at[i])
+        both = own[i] + xrecv[i].astype(F32)
+        own[i] = both
+        zsend[i] = both.astype(BF16)
+        for r in range(4) if i < 3 else (2, 3, 1):
+            zt = q * 4 + r if i < 3 else z ^ r
+            piece = zsend.at[i, pl.ds(pl.multiple_of((zt % 4) * R, R), R)]
+            send(piece, zrecv.at[z], z_send.at[k], z_recv, dev(d, xh * NZ + zt))
+            k += 1
 
     climb(lrun, lgot, l_send, l_recv, 3)
     climb(lrun, lgot, l_send, l_recv, 4)
     loss = jnp.sum(lrun[4], axis=1, keepdims=True) / count
     row_ref[2:3] = jnp.broadcast_to(loss, (1, TOK))
 
-    kept = own[z // 4, pl.ds(pl.multiple_of((z % 4) * R, R), R), :]
+    kept = own[3, pl.ds(pl.multiple_of((z % 4) * R, R), R), :]
     arrived(zrecv.at[pl.ds(0, 15)], z_recv)
     for r in range(1, 16):
         kept = kept + zrecv[z ^ r].astype(F32)
     grad_ref[...] = kept.astype(BF16)
-    for zt, copy in elsewhere:
-        pl.when(z != zt)(copy.wait_send)
     for copy in started:
         copy.wait_send()
 
@@ -443,7 +446,7 @@
             pltpu.VMEM((TOK, VT), BF16),
             pltpu.VMEM((1, TOK), jnp.int32),
             pltpu.VMEM((1, TOK), jnp.int32),
-            dma((48,)), dma((34,)), dma((32,)), dma((32,)), dma((5,)), dma((16,)), dma((2,)),
+            dma((48,)), dma((34,)), dma((32,)), dma((32,)), dma((5,)), dma((16,)), dma((4,)),
             dma((31,)), dma, dma((4,)), dma((4,)), dma((4,)), dma((4,)), dma((4,)), dma((4,)), dma((16,)), dma,
             pltpu.SemaphoreType.REGULAR((4,)),
         ],

time: 88.9 us -> 83.8 us (0.943)
  the two profiles are of different devices: /device:TPU:66 before, /device:TPU:64 now
where the time goes in v3:
time: 83.8 us; the launch traced here: 83.5 us
  Pallas kernels  82.9 us (99%)
    pallas_call x1, Pallas kernels, on_device(): pl.pallas_call(kernel, out_shape=(jax.ShapeDtypeStruct((R, TOK), BF16), j...  81.6 us

profile of v3, /device:TPU:64, one launch (start us, length us, event | category | flops | bytes accessed | tf_op | source)
XLA Modules:
  0.0 83.5 jit_solution(234130120683541875)
XLA Ops:
  0.6 81.6 %shard_map.84 = (bf16[64,128]{1,0:T(8,128)(2,1)}, f32[8,128]{1,0:T(8,128)}) custom-call(bf16[64,128]{1,0:T(8,128)(2,1)} %bitcast.7, bf16[64,4864]{1,0:T(8,128)(2,1)} %bitcast.6, bf16[128,2432]{1,0:T(8,128)(2,1)} %tea_hbm.1, s32[1,128]{1,0:T(1,128)} %bitcast.8, s32[1,128]{1,0:T(1,128)} %bitcast.9), custom_call_target="tpu_custom_call" | custom-call | tf_op jit(solution)/shard_map/pallas_call | solution.py:422
  82.2 1.3 %shard_map.85 = (bf16[64,128]{1,0:T(8,128)(2,1)}, f32[128]{0:T(128)}, f32[128]{0:T(128)}, f32[1,1]{1,0:T(1,128)}) custom-call(bf16[64,128]{1,0:T(8,128)(2,1)} %get-tuple-element.10.grad_in, f32[8,128]{1,0:T(8,128)} %get-tuple-element.11.row_in), custom_call_target="tpu_custom_call" | custom-call | tf_op jit(solution)/shard_map/pallas_call | solution.py:457

commit v4 on v3

--- a/solution.py
+++ b/solution.py
@@ -12,9 +12,9 @@
 TOK = 128
 R = 64
 NT = VT // 128
-CUT = 1280
-COLS = (pl.ds(0, CUT), pl.ds(CUT, VT - CUT))
-TILES = (range(CUT // 128), range(CUT // 128, NT))
+CUTS = (0, 1280, 2048, VT)
+COLS = tuple(pl.ds(a, b - a) for a, b in zip(CUTS, CUTS[1:]))
+TILES = tuple(range(a // 128, b // 128) for a, b in zip(CUTS, CUTS[1:]))
 NZ = 16
 MESH = pl.DeviceIdType.MESH
 
@@ -24,10 +24,10 @@
 def kernel(
     hid_hbm, blk_ref, tea_hbm, ids_hbm, mask_hbm,
     grad_ref, row_ref,
-    w, ht, hg, acc, lt, tt, et, dl, stat, mrun, mgot, lrun, lgot, xsend, xrecv, own, zsend, zrecv,
+    w, ht, hg, acc, lt, tt, et, dl, stat, tstat, away, mrun, mgot, lrun, lgot, xsend, xrecv, own, zsend, zrecv,
     tea_ref, ids_ref, mask_ref,
     w_send, w_recv, d_send, d_recv, loc_sem, h_send, h_recv,
-    s_send, s_recv, m_send, m_recv, l_send, l_recv, x_send, x_recv, z_send, z_recv, ready,
+    s_send, s_recv, t_send, t_recv, m_send, m_recv, l_send, l_recv, x_send, x_recv, z_send, z_recv, ready,
 ):
     d = lax.axis_index("dp")
     v = lax.axis_index("vocab")
@@ -58,25 +58,27 @@
     for to in (target[YP], target[YM], target[XP], target[CP], along_z(1), along_z(15), across_x):
         pl.semaphore_signal(barrier, inc=1, device_id=to, device_id_type=MESH)
     near = blk_ref.at[:, pl.ds(pl.multiple_of(h * VT, 128), VT)]
-    away = blk_ref.at[:, pl.ds(pl.multiple_of((1 - h) * VT, 128), VT)]
+    rest = blk_ref.at[:, pl.ds(pl.multiple_of((1 - h) * VT, 128), VT)]
     own_rows = pl.ds(pl.multiple_of(h * 1024 + R * d, R), R)
     fetches = [
         pltpu.make_async_copy(src, dst, loc_sem.at[i])
         for i, (src, dst) in enumerate(
             [
+                (near, w.at[own_rows]),
+                (rest, away),
                 (hid_hbm, ht.at[z, mine]),
                 (mask_hbm, mask_ref),
                 (tea_hbm, tea_ref),
                 (ids_hbm, ids_ref),
-                (near, w.at[own_rows]),
             ]
         )
     ]
     for fetch in fetches:
         fetch.start()
-    fetches[0].wait()
-    fetches[1].wait()
+    fetches[3].wait()
     mrun[0] = mask_ref[...].astype(F32)
+    for fetch in fetches[:3]:
+        fetch.wait()
     pl.semaphore_wait(barrier, 7)
 
     started = []
@@ -103,18 +105,18 @@
             send(run.at[step], got.at[step], ssem.at[step], rsem.at[step], ladder[step])
 
     def unit(u, dx, dy, core, sub=None):
-        base = (h ^ (u // 2)) * 1024 + R * ((xl ^ dx) * 8 + ((y + dy) % 4) * 2 + core)
+        base = (h ^ (u // 3)) * 1024 + R * ((xl ^ dx) * 8 + ((y + dy) % 4) * 2 + core)
         if sub is None:
-            return w.at[pl.ds(pl.multiple_of(base, R), R), COLS[u % 2]]
-        return w.at[pl.ds(pl.multiple_of(base + 32 * sub, 32), 32), COLS[u % 2]]
+            return w.at[pl.ds(pl.multiple_of(base, R), R), COLS[u % 3]]
+        return w.at[pl.ds(pl.multiple_of(base + 32 * sub, 32), 32), COLS[u % 3]]
 
     counter = {"w": 0, "d": 0}
-    subs = {(0, 1, 1, 0): 32, (0, 1, 3, 1): 33, (0, 1, 1, 1): None, (0, 1, 3, 0): None}
+    subs = {(0, 1, 1, 0): 48, (0, 1, 3, 1): 49, (0, 1, 1, 1): None, (0, 1, 3, 0): None}
 
     def sem_of(u, dx, dy, sub=None):
         return subs.get((u, dx, dy, sub)) or u * 8 + dx * 4 + dy
 
-    def pass_on(u, dx, dy, way, sub=None, src=None):
+    def pass_on(u, dx, dy, way, sub=None):
         ref = unit(u, dx, dy, c, sub)
         if way == XP:
             at = (u, dx ^ 1, dy, sub)
@@ -124,7 +126,7 @@
             at = (u, dx, (dy + 1) % 4, sub)
         k = counter["w"]
         counter["w"] += 1
-        send(ref if src is None else src, ref, w_send.at[k], w_recv.at[sem_of(*at)], target[way])
+        send(ref, ref, w_send.at[k], w_recv.at[sem_of(*at)], target[way])
 
     def across(u, dx, dy):
         ref = unit(u, dx, dy, c)
@@ -137,19 +139,20 @@
 
     def peer_in(u, dx):
         for dy in range(4):
-            if (u, dx, dy) not in ((0, 0, 0), (1, 0, 0)):
+            if (u, dx, dy) not in ((0, 0, 0), (1, 0, 0), (2, 0, 0)):
                 arrived(unit(u, dx, dy, 1 - c), d_recv.at[sem_of(u, dx, dy)])
 
-    for u in (0, 1):
+    for u in (0, 1, 2):
         for way in (XP, YP, YM):
-            pass_on(u, 0, 0, way, src=near.at[:, COLS[u]])
-        send(away.at[:, COLS[u]], w.at[own_rows, COLS[u]], w_send.at[46 + u], w_recv.at[sem_of(2 + u, 0, 0)], target[ZP])
+            pass_on(u, 0, 0, way)
+        send(away.at[:, COLS[u]], w.at[own_rows, COLS[u]], w_send.at[45 + u], w_recv.at[sem_of(3 + u, 0, 0)], target[ZP])
     send(ht.at[z, mine], ht.at[z, mine], h_send.at[15], h_recv.at[1], across_x)
-    send(near, w.at[own_rows], d_send.at[31], d_recv.at[0], target[CP])
+    send(w.at[own_rows], w.at[own_rows], d_send.at[47], d_recv.at[0], target[CP])
     tell(0, along_z(1), along_z(15))
     climb(mrun, mgot, m_send, m_recv, 0)
 
-    fetches[2].wait()
+    fetches[4].wait()
+
     def fold(block, how):
         return how(block.reshape(16, 8, 128), axis=0)
 
@@ -173,6 +176,7 @@
         et[tile(j), :] = e
         total = total + fold(e, jnp.sum)
     t_sum = total.sum(axis=0, keepdims=True)
+    tstat[v] = jnp.concatenate([t_max, t_sum], axis=0)
     climb(mrun, mgot, m_send, m_recv, 1)
 
     hidden = iter(range(15))
@@ -193,69 +197,73 @@
     across(0, 0, 3)
     piece_in(0, 0, 1)
     across(0, 0, 1)
-    piece_in(2, 0, 0)
-    pass_on(2, 0, 0, XP)
-    pass_on(2, 0, 0, YP)
-    pass_on(2, 0, 0, YM)
+    piece_in(3, 0, 0)
+    pass_on(3, 0, 0, XP)
+    pass_on(3, 0, 0, YP)
+    pass_on(3, 0, 0, YM)
     pass_on(0, 0, 3, XP, sub=1)
     pass_on(0, 0, 1, XP, sub=0)
-    across(2, 0, 0)
+    across(3, 0, 0)
     piece_in(0, 1, 0)
     across(0, 1, 0)
     climb(mrun, mgot, m_send, m_recv, 2)
-    piece_in(1, 0, 1)
-    pass_on(1, 0, 1, YM)
-    across(1, 0, 1)
-    piece_in(1, 0, 3)
-    across(1, 0, 3)
-    piece_in(3, 0, 0)
-    pass_on(3, 0, 0, YP)
-    pass_on(3, 0, 0, YM)
-    pass_on(3, 0, 0, XP)
-    across(3, 0, 0)
-    piece_in(1, 1, 0)
-    across(1, 1, 0)
+    for u in (1, 2):
+        piece_in(u, 0, 1)
+        pass_on(u, 0, 1, YM)
+        across(u, 0, 1)
+        piece_in(u, 0, 3)
+        across(u, 0, 3)
+    for u in (4, 5):
+        piece_in(u, 0, 0)
+        pass_on(u, 0, 0, YP)
+        pass_on(u, 0, 0, YM)
+        pass_on(u, 0, 0, XP)
+        across(u, 0, 0)
+    for u in (1, 2):
+        piece_in(u, 1, 0)
+        across(u, 1, 0)
     piece_in(0, 0, 2)
     pass_on(0, 0, 2, XP)
     across(0, 0, 2)
-    piece_in(2, 0, 1)
-    across(2, 0, 1)
-    piece_in(2, 1, 0)
-    across(2, 1, 0)
+    piece_in(3, 0, 1)
+    across(3, 0, 1)
+    piece_in(3, 1, 0)
+    across(3, 1, 0)
     climb(mrun, mgot, m_send, m_recv, 3)
-    piece_in(2, 0, 3)
-    pass_on(2, 0, 3, YP)
-    across(2, 0, 3)
-    piece_in(1, 0, 2)
-    pass_on(1, 0, 2, XP)
-    across(1, 0, 2)
+    piece_in(3, 0, 3)
+    pass_on(3, 0, 3, YP)
+    across(3, 0, 3)
+    for u in (1, 2):
+        piece_in(u, 0, 2)
+        pass_on(u, 0, 2, XP)
+        across(u, 0, 2)
     before, after = (z + 12) % NZ, (z + 4) % NZ
     arrived(ht.at[before], h_recv.at[2])
     spread(before, 4, 3, 2, 1)
     arrived(ht.at[after], h_recv.at[3])
     spread(after, 13, 14, 15)
-    piece_in(3, 0, 1)
-    pass_on(3, 0, 1, YM)
-    across(3, 0, 1)
-    for u in (0, 1, 2):
+    for u in (4, 5):
+        piece_in(u, 0, 1)
+        pass_on(u, 0, 1, YM)
+        across(u, 0, 1)
+    for u in (0, 1, 2, 3):
         pass_on(u, 1, 0, YP, sub=None if u else 0)
         pass_on(u, 1, 0, YM, sub=None if u else 1)
-    piece_in(3, 0, 3)
-    across(3, 0, 3)
-    piece_in(3, 1, 0)
-    pass_on(3, 1, 0, YP)
-    pass_on(3, 1, 0, YM)
-    across(3, 1, 0)
-    piece_in(2, 0, 2)
-    pass_on(2, 0, 2, XP)
-    across(2, 0, 2)
-    piece_in(3, 0, 2)
-    pass_on(3, 0, 2, XP)
-    across(3, 0, 2)
+    for u in (4, 5):
+        piece_in(u, 0, 3)
+        across(u, 0, 3)
+    for u in (4, 5):
+        piece_in(u, 1, 0)
+        pass_on(u, 1, 0, YP)
+        pass_on(u, 1, 0, YM)
+        across(u, 1, 0)
+    for u in (3, 4, 5):
+        piece_in(u, 0, 2)
+        pass_on(u, 0, 2, XP)
+        across(u, 0, 2)
     piece_in(0, 1, 2)
     across(0, 1, 2)
     climb(mrun, mgot, m_send, m_recv, 4)
-
     pl.semaphore_wait(ready.at[2], 2)
     tell(3, across_x)
 
@@ -265,11 +273,11 @@
         hg[g] = part.reshape(512, TOK).astype(F32).T.astype(BF16)
 
     def multiply(u, dx):
-        g = (h ^ (u // 2)) * 2 + (xl ^ dx)
+        g = (h ^ (u // 3)) * 2 + (xl ^ dx)
         rows = pl.ds(pl.multiple_of(g * 512, 512), 512)
-        cols = COLS[u % 2]
+        cols = COLS[u % 3]
         part = jnp.dot(hg[g], w[rows, cols], preferred_element_type=F32)
-        acc[:, cols] = part if (u // 2, dx) == (0, 0) else acc[:, cols] + part
+        acc[:, cols] = part if (u // 3, dx) == (0, 0) else acc[:, cols] + part
 
     def statistics(p):
         top, hit = low8, zero8
@@ -289,82 +297,91 @@
             cross = cross + fold(et[tile(j), :] * (tt[tile(j), :] - logit), jnp.sum)
         return high, *(a.sum(axis=0, keepdims=True) for a in (total, cross, hit))
 
-    fetches[3].wait()
+    fetches[5].wait()
     ids = ids_ref[...]
-    fetches[4].wait()
     other_rows = pl.ds(pl.multiple_of(h * 1024 + R * (d ^ 1), R), R)
     arrived(w.at[other_rows], d_recv.at[0])
-    for u in (0, 1):
+    for u in (0, 1, 2):
         peer_in(u, 0)
         multiply(u, 0)
+    everybody = []
+    for offset in far + [0]:
+        for other in (1, 0):
+            if other or offset:
+                everybody.append(dev(d, (xh ^ other) * NZ + (z + offset) % NZ))
+    pl.semaphore_wait(ready.at[3], 1)
+    for k, to in enumerate(everybody):
+        send(tstat.at[v], tstat.at[v], t_send.at[k], t_recv, to)
     for dy in (3, 1):
         for sub in (0, 1):
             piece_in(0, 1, dy, sub)
         across(0, 1, dy)
-    for u in (2, 3):
+    for u in (3, 4, 5):
         peer_in(u, 0)
         multiply(u, 0)
-    for dy in (2, 3, 1):
-        piece_in(1, 1, dy)
-        across(1, 1, dy)
+    for u in (1, 2):
+        for dy in (2, 3, 1):
+            piece_in(u, 1, dy)
+            across(u, 1, dy)
     peer_in(0, 1)
     multiply(0, 1)
     for dy in (2, 3, 1):
-        piece_in(2, 1, dy)
-        across(2, 1, dy)
-    peer_in(1, 1)
-    multiply(1, 1)
-    peer_in(2, 1)
-    multiply(2, 1)
-    piece_in(3, 1, 2)
-    across(3, 1, 2)
-    max_0, sum_0, cross_0, hit_0 = statistics(0)
-    for dy in (3, 1):
         piece_in(3, 1, dy)
         across(3, 1, dy)
-    pl.semaphore_wait(ready.at[3], 1)
+    for u in (1, 2):
+        peer_in(u, 1)
+        multiply(u, 1)
+    for u in (4, 5):
+        piece_in(u, 1, 2)
+        across(u, 1, 2)
     peer_in(3, 1)
     multiply(3, 1)
-    max_1, sum_1, cross_1, hit_1 = statistics(1)
-    s_max = jnp.maximum(max_0, max_1)
-    s_sum = sum_0 * jnp.exp(max_0 - s_max) + sum_1 * jnp.exp(max_1 - s_max)
-    x_sum = cross_0 + cross_1
-    s_hit = hit_0 + hit_1
-    stat[v] = jnp.concatenate([t_max, s_max, t_sum, x_sum, s_sum, s_hit, s_hit, s_hit], axis=0)
-
-    k = 0
-    for offset in far + [0]:
-        for other in (1, 0):
-            if other or offset:
-                to = dev(d, (xh ^ other) * NZ + (z + offset) % NZ)
-                send(stat.at[v], stat.at[v], s_send.at[k], s_recv, to)
-                k += 1
+    parts = [statistics(0)]
+    for u in (4, 5):
+        for dy in (3, 1):
+            piece_in(u, 1, dy)
+            across(u, 1, dy)
+    for u in (4, 5):
+        peer_in(u, 1)
+        multiply(u, 1)
+        parts.append(statistics(u - 3))
+    maxima = [part[0] for part in parts]
+    s_max = jnp.maximum(jnp.maximum(maxima[0], maxima[1]), maxima[2])
+    s_sum = sum(part[1] * jnp.exp(part[0] - s_max) for part in parts)
+    x_sum = sum(part[2] for part in parts)
+    s_hit = sum(part[3] for part in parts)
+    stat[v] = jnp.concatenate([s_max, s_sum, x_sum, s_hit], axis=0)
+    for k, to in enumerate(everybody):
+        send(stat.at[v], stat.at[v], s_send.at[k], s_recv, to)
+    arrived(tstat.at[pl.ds(0, 31)], t_recv)
     count = jnp.sum(mrun[4], axis=1, keepdims=True)
     factor = mask_ref[...].astype(F32) / count
+    t_top = tstat[0][0:1]
+    for r in range(1, 32):
+        t_top = jnp.maximum(t_top, tstat[r][0:1])
+    t_scales = [jnp.exp(tstat[r][0:1] - t_top) for r in range(32)]
+    tz = sum(t_scales[r] * tstat[r][1:2] for r in range(32))
+    t_lse = t_top + jnp.log(tz)
+    t_scale = factor * (jnp.exp(t_max - t_top) / tz)
     arrived(stat.at[pl.ds(0, 31)], s_recv)
-    tops = stat[0]
+    tops = stat[0][0:1]
     for r in range(1, 32):
-        tops = jnp.maximum(tops, stat[r])
-    tops = tops[0:2]
-    tz = xz = sz = hz = jnp.zeros((1, 128), F32)
+        tops = jnp.maximum(tops, stat[r][0:1])
+    xz = sz = hz = jnp.zeros((1, 128), F32)
     for r in range(32):
         one = stat[r]
-        scale = jnp.exp(one[0:2] - tops)
-        tz = tz + scale[0:1] * one[2:3]
-        xz = xz + scale[0:1] * one[3:4]
-        sz = sz + scale[1:2] * one[4:5]
-        hz = hz + one[5:6]
-    t_lse = tops[0:1] + jnp.log(tz)
-    s_lse = tops[1:2] + jnp.log(sz)
+        sz = sz + jnp.exp(one[0:1] - tops) * one[1:2]
+        xz = xz + t_scales[r] * one[2:3]
+        hz = hz + one[3:4]
+    s_lse = tops + jnp.log(sz)
     kl = xz / tz - t_lse + s_lse
     row_ref[0:1] = kl
     row_ref[1:2] = hz - s_lse
     lrun[0] = kl * mask_ref[...].astype(F32)
     climb(lrun, lgot, l_send, l_recv, 0)
 
-    t_scale = factor * (jnp.exp(t_max - tops[0:1]) / tz)
-    for p, high in enumerate((max_0, max_1)):
-        s_scale = factor * (jnp.exp(high - tops[1:2]) / sz)
+    for p, high in enumerate(maxima):
+        s_scale = factor * (jnp.exp(high - tops) / sz)
         for j in TILES[p]:
             dl[tile(j), :] = (lt[tile(j), :] * s_scale - et[tile(j), :] * t_scale).astype(BF16)
 
@@ -433,7 +450,9 @@
             pltpu.VMEM((VT, TOK), F32),
             pltpu.VMEM((VT, TOK), F32),
             pltpu.VMEM((VT, TOK), BF16),
-            pltpu.VMEM((32, 8, TOK), F32),
+            pltpu.VMEM((32, 4, TOK), F32),
+            pltpu.VMEM((32, 2, TOK), F32),
+            pltpu.VMEM((R, VT), BF16),
             pltpu.VMEM((5, 1, TOK), F32),
             pltpu.VMEM((4, 1, TOK), F32),
             pltpu.VMEM((5, 1, TOK), F32),
@@ -446,8 +465,8 @@
             pltpu.VMEM((TOK, VT), BF16),
             pltpu.VMEM((1, TOK), jnp.int32),
             pltpu.VMEM((1, TOK), jnp.int32),
-            dma((48,)), dma((34,)), dma((32,)), dma((32,)), dma((5,)), dma((16,)), dma((4,)),
-            dma((31,)), dma, dma((4,)), dma((4,)), dma((4,)), dma((4,)), dma((4,)), dma((4,)), dma((16,)), dma,
+            dma((48,)), dma((50,)), dma((48,)), dma((48,)), dma((6,)), dma((16,)), dma((4,)),
+            dma((31,)), dma, dma((31,)), dma, dma((4,)), dma((4,)), dma((4,)), dma((4,)), dma((4,)), dma((4,)), dma((16,)), dma,
             pltpu.SemaphoreType.REGULAR((4,)),
         ],
         compiler_params=pltpu.CompilerParams(

time: 83.8 us -> 82.4 us (0.983)
  the two profiles are of different devices: /device:TPU:64 before, /device:TPU:2 now
where the time goes in v4:
time: 82.4 us; the launch traced here: 82.2 us
  Pallas kernels  81.6 us (99%)
    pallas_call x1, Pallas kernels, on_device(): pl.pallas_call(kernel, out_shape=(jax.ShapeDtypeStruct((R, TOK), BF16), j...  80.3 us

profile of v4, /device:TPU:2, one launch (start us, length us, event | category | flops | bytes accessed | tf_op | source)
XLA Modules:
  0.0 82.2 jit_solution(3867855388896634)
XLA Ops:
  0.6 80.3 %shard_map.84 = (bf16[64,128]{1,0:T(8,128)(2,1)}, f32[8,128]{1,0:T(8,128)}) custom-call(bf16[64,128]{1,0:T(8,128)(2,1)} %bitcast.7, bf16[64,4864]{1,0:T(8,128)(2,1)} %bitcast.6, bf16[128,2432]{1,0:T(8,128)(2,1)} %tea_hbm.1, s32[1,128]{1,0:T(1,128)} %bitcast.8, s32[1,128]{1,0:T(1,128)} %bitcast.9), custom_call_target="tpu_custom_call" | custom-call | tf_op jit(solution)/shard_map/pallas_call | solution.py:439
  80.9 1.3 %shard_map.85 = (bf16[64,128]{1,0:T(8,128)(2,1)}, f32[128]{0:T(128)}, f32[128]{0:T(128)}, f32[1,1]{1,0:T(1,128)}) custom-call(bf16[64,128]{1,0:T(8,128)(2,1)} %get-tuple-element.10.grad_in, f32[8,128]{1,0:T(8,128)} %get-tuple-element.11.row_in), custom_call_target="tpu_custom_call" | custom-call | tf_op jit(solution)/shard_map/pallas_call | solution.py:476

commit v5 on v4

--- a/solution.py
+++ b/solution.py
@@ -24,10 +24,10 @@
 def kernel(
     hid_hbm, blk_ref, tea_hbm, ids_hbm, mask_hbm,
     grad_ref, row_ref,
-    w, ht, hg, acc, lt, tt, et, dl, stat, tstat, away, mrun, mgot, lrun, lgot, xsend, xrecv, own, zsend, zrecv,
+    w, ht, hg, acc, lt, tt, et, dl, stat, tstat, away, mrun, mgot, lrun, lgot, xsend, xrecv, own, zsend, zrecv, feed, zagg,
     tea_ref, ids_ref, mask_ref,
     w_send, w_recv, d_send, d_recv, loc_sem, h_send, h_recv,
-    s_send, s_recv, t_send, t_recv, m_send, m_recv, l_send, l_recv, x_send, x_recv, z_send, z_recv, ready,
+    s_send, s_recv, t_send, t_recv, m_send, m_recv, l_send, l_recv, x_send, x_recv, z_send, z_recv, f_recv, ready,
 ):
     d = lax.axis_index("dp")
     v = lax.axis_index("vocab")
@@ -385,42 +385,51 @@
         for j in TILES[p]:
             dl[tile(j), :] = (lt[tile(j), :] * s_scale - et[tile(j), :] * t_scale).astype(BF16)
 
-    def quarter(half, q):
-        rows = pl.ds(pl.multiple_of(half * 1024 + q * 256, 256), 256)
-        return jnp.dot(w[rows, :], dl[...], preferred_element_type=F32)
-
-    zq = z // 4
-    first, second = 2 * ((3 - zq) // 3), 3 - 2 * (zq // 2)
-    order = (first, second, 6 - first - second - zq, zq)
-    for i, q in enumerate(order):
-        xsend[i] = quarter(1 - xh, q).astype(BF16)
+    groups = ((8, 7, 9, 6), (10, 5, 11, 4), (12, 3, 13, 2), (14, 1, 15, 0))
+    feeds = {8: (4, 0), 7: (3, 1), 6: (2, 2), 5: (1, 3), 9: (13, 4), 10: (14, 5), 11: (15, 6)}
+    slots = {4: 0, 12: 1, 3: 2, 13: 3, 2: 4, 14: 5, 1: 6, 15: 7}
+
+    def blocks_of(half, group):
+        lines = [w[pl.ds(pl.multiple_of(half * 1024 + ((z + k) % NZ) * R, R), R), :] for k in group]
+        return jnp.dot(jnp.concatenate(lines, axis=0), dl[...], preferred_element_type=F32)
+
+    for i, group in enumerate(groups):
+        xsend[i] = blocks_of(1 - xh, group).astype(BF16)
         send(xsend.at[i], xrecv.at[i], x_send.at[i], x_recv.at[i], across_x)
     climb(lrun, lgot, l_send, l_recv, 1)
-    for i, q in enumerate(order):
-        own[i] = quarter(xh, q)
-    climb(lrun, lgot, l_send, l_recv, 2)
-    k = 0
-    for i, q in enumerate(order):
+    for i, group in enumerate(groups):
+        own[i] = blocks_of(xh, group)
+    links = iter(range(15))
+    for i, group in enumerate(groups):
         arrived(xrecv.at[i], x_recv.at[i])
         both = own[i] + xrecv[i].astype(F32)
         own[i] = both
         zsend[i] = both.astype(BF16)
-        for r in range(4) if i < 3 else (2, 3, 1):
-            zt = q * 4 + r if i < 3 else z ^ r
-            piece = zsend.at[i, pl.ds(pl.multiple_of((zt % 4) * R, R), R)]
-            send(piece, zrecv.at[z], z_send.at[k], z_recv, dev(d, xh * NZ + zt))
-            k += 1
+        for r, step in enumerate(group):
+            piece = zsend.at[i, pl.ds(r * R, R)]
+            if step in feeds:
+                node, slot = feeds[step]
+                send(piece, feed.at[slot], z_send.at[next(links)], f_recv.at[slot // 4], along_z(node))
+            elif step not in (0, 4, 12):
+                send(piece, zrecv.at[slots[step]], z_send.at[next(links)], z_recv, along_z(step))
+        if i == 1:
+            climb(lrun, lgot, l_send, l_recv, 2)
+    for side, (step, kept, count_in) in enumerate(((4, own[1, 3 * R :, :], 4), (12, own[2, :R, :], 3))):
+        arrived(feed.at[pl.ds(4 * side, count_in)], f_recv.at[side])
+        for slot in range(count_in):
+            kept = kept + feed[4 * side + slot].astype(F32)
+        zagg[side] = kept.astype(BF16)
+        send(zagg.at[side], zrecv.at[slots[step]], z_send.at[next(links)], z_recv, along_z(step))
 
     climb(lrun, lgot, l_send, l_recv, 3)
+    kept = own[3, 3 * R :, :]
+    arrived(zrecv, z_recv)
+    for slot in range(8):
+        kept = kept + zrecv[slot].astype(F32)
+    grad_ref[...] = kept.astype(BF16)
     climb(lrun, lgot, l_send, l_recv, 4)
     loss = jnp.sum(lrun[4], axis=1, keepdims=True) / count
     row_ref[2:3] = jnp.broadcast_to(loss, (1, TOK))
-
-    kept = own[3, pl.ds(pl.multiple_of((z % 4) * R, R), R), :]
-    arrived(zrecv.at[pl.ds(0, 15)], z_recv)
-    for r in range(1, 16):
-        kept = kept + zrecv[z ^ r].astype(F32)
-    grad_ref[...] = kept.astype(BF16)
     for copy in started:
         copy.wait_send()
 
@@ -461,12 +470,14 @@
             pltpu.VMEM((4, 256, TOK), BF16),
             pltpu.VMEM((4, 256, TOK), F32),
             pltpu.VMEM((4, 256, TOK), BF16),
-            pltpu.VMEM((NZ, R, TOK), BF16),
+            pltpu.VMEM((8, R, TOK), BF16),
+            pltpu.VMEM((7, R, TOK), BF16),
+            pltpu.VMEM((2, R, TOK), BF16),
             pltpu.VMEM((TOK, VT), BF16),
             pltpu.VMEM((1, TOK), jnp.int32),
             pltpu.VMEM((1, TOK), jnp.int32),
             dma((48,)), dma((50,)), dma((48,)), dma((48,)), dma((6,)), dma((16,)), dma((4,)),
-            dma((31,)), dma, dma((31,)), dma, dma((4,)), dma((4,)), dma((4,)), dma((4,)), dma((4,)), dma((4,)), dma((16,)), dma,
+            dma((31,)), dma, dma((31,)), dma, dma((4,)), dma((4,)), dma((4,)), dma((4,)), dma((4,)), dma((4,)), dma((16,)), dma, dma((2,)),
             pltpu.SemaphoreType.REGULAR((4,)),
         ],
         compiler_params=pltpu.CompilerParams(

time: 82.4 us -> 81.2 us (0.985)
  Pallas kernels: 81.6 us -> 80.3 us
    pallas_call x1, Pallas kernels: 80.3 us -> 79 us  [on_device(): pl.pallas_call(kernel, out_shape=(jax.ShapeDtypeStruct((R, TOK), BF16), j...]
where the time goes in v5:
time: 81.2 us; the launch traced here: 81 us
  Pallas kernels  80.3 us (99%)
    pallas_call x1, Pallas kernels, on_device(): pl.pallas_call(kernel, out_shape=(jax.ShapeDtypeStruct((R, TOK), BF16), j...  79 us

profile of v5, /device:TPU:2, one launch (start us, length us, event | category | flops | bytes accessed | tf_op | source)
XLA Modules:
  0.0 81.0 jit_solution(5803190793379005584)
XLA Ops:
  0.6 79.0 %shard_map.84 = (bf16[64,128]{1,0:T(8,128)(2,1)}, f32[8,128]{1,0:T(8,128)}) custom-call(bf16[64,128]{1,0:T(8,128)(2,1)} %bitcast.7, bf16[64,4864]{1,0:T(8,128)(2,1)} %bitcast.6, bf16[128,2432]{1,0:T(8,128)(2,1)} %tea_hbm.1, s32[1,128]{1,0:T(1,128)} %bitcast.8, s32[1,128]{1,0:T(1,128)} %bitcast.9), custom_call_target="tpu_custom_call" | custom-call | tf_op jit(solution)/shard_map/pallas_call | solution.py:448
  79.6 1.3 %shard_map.85 = (bf16[64,128]{1,0:T(8,128)(2,1)}, f32[128]{0:T(128)}, f32[128]{0:T(128)}, f32[1,1]{1,0:T(1,128)}) custom-call(bf16[64,128]{1,0:T(8,128)(2,1)} %get-tuple-element.10.grad_in, f32[8,128]{1,0:T(8,128)} %get-tuple-element.11.row_in), custom_call_target="tpu_custom_call" | custom-call | tf_op jit(solution)/shard_map/pallas_call | solution.py:487

commit v6 on v5

--- a/solution.py
+++ b/solution.py
@@ -12,7 +12,7 @@
 TOK = 128
 R = 64
 NT = VT // 128
-CUTS = (0, 1280, 2048, VT)
+CUTS = (0, 1280, 2176, VT)
 COLS = tuple(pl.ds(a, b - a) for a, b in zip(CUTS, CUTS[1:]))
 TILES = tuple(range(a // 128, b // 128) for a, b in zip(CUTS, CUTS[1:]))
 NZ = 16
@@ -414,7 +414,7 @@
                 send(piece, zrecv.at[slots[step]], z_send.at[next(links)], z_recv, along_z(step))
         if i == 1:
             climb(lrun, lgot, l_send, l_recv, 2)
-    for side, (step, kept, count_in) in enumerate(((4, own[1, 3 * R :, :], 4), (12, own[2, :R, :], 3))):
+    for side, step, kept, count_in in ((1, 12, own[2, :R, :], 3), (0, 4, own[1, 3 * R :, :], 4)):
         arrived(feed.at[pl.ds(4 * side, count_in)], f_recv.at[side])
         for slot in range(count_in):
             kept = kept + feed[4 * side + slot].astype(F32)

time: 81.2 us -> 79.8 us (0.983)
  Pallas kernels: 80.3 us -> 78.9 us
    pallas_call x1, Pallas kernels: 79 us -> 77.5 us  [on_device(): pl.pallas_call(kernel, out_shape=(jax.ShapeDtypeStruct((R, TOK), BF16), j...]
where the time goes in v6:
time: 79.8 us; the launch traced here: 79.5 us
  Pallas kernels  78.9 us (99%)
    pallas_call x1, Pallas kernels, on_device(): pl.pallas_call(kernel, out_shape=(jax.ShapeDtypeStruct((R, TOK), BF16), j...  77.5 us

profile of v6, /device:TPU:2, one launch (start us, length us, event | category | flops | bytes accessed | tf_op | source)
XLA Modules:
  0.0 79.5 jit_solution(506312001051557649)
XLA Ops:
  0.6 77.5 %shard_map.84 = (bf16[64,128]{1,0:T(8,128)(2,1)}, f32[8,128]{1,0:T(8,128)}) custom-call(bf16[64,128]{1,0:T(8,128)(2,1)} %bitcast.7, bf16[64,4864]{1,0:T(8,128)(2,1)} %bitcast.6, bf16[128,2432]{1,0:T(8,128)(2,1)} %tea_hbm.1, s32[1,128]{1,0:T(1,128)} %bitcast.8, s32[1,128]{1,0:T(1,128)} %bitcast.9), custom_call_target="tpu_custom_call" | custom-call | tf_op jit(solution)/shard_map/pallas_call | solution.py:448
  78.2 1.3 %shard_map.85 = (bf16[64,128]{1,0:T(8,128)(2,1)}, f32[128]{0:T(128)}, f32[128]{0:T(128)}, f32[1,1]{1,0:T(1,128)}) custom-call(bf16[64,128]{1,0:T(8,128)(2,1)} %get-tuple-element.10.grad_in, f32[8,128]{1,0:T(8,128)} %get-tuple-element.11.row_in), custom_call_target="tpu_custom_call" | custom-call | tf_op jit(solution)/shard_map/pallas_call | solution.py:487
